TPU v7x, 128 devices: a whole 4x4x4 slice. The times are simulated.
128 devices in a mesh: batch: 1, rows: 128 (over z, y, x, core).
Axes of the slice: x: 4, y: 4, z: 4, core: 2. Of those that a mesh axis runs over, the one named last changes fastest.
Arguments:
- a_mat: float32 [524288, 512], P(('batch', 'rows'))
- rhs: float32 [524288, 128], P(('batch', 'rows'))
Outputs:
- output 1: float32 [512, 128], P('batch')
- output 2: float32 [512, 512], P('batch')
All inputs are finite; a program needn't handle non-finite values.
Results may differ from a plain program's by a relative error of at most 0.001.
Values sent between devices are 32-bit elements.
A program may use at most 1 GiB of HBM per device.

v0:
```python
import jax
import jax.numpy as jnp
from jax import lax
from jax.sharding import PartitionSpec as P

HIGHEST = lax.Precision.HIGHEST


def gram_of(left_mat, right_mat):
    return lax.dot_general(left_mat, right_mat, (((0,), (0,)), ((), ())), precision=HIGHEST, preferred_element_type=jnp.float32)


def solution(mesh):
    def group_solve(a_blk, b_blk):
        gram_one = lax.psum(gram_of(a_blk, a_blk), "rows")
        low_one = jnp.linalg.cholesky(gram_one)
        q_one = lax.linalg.triangular_solve(low_one, a_blk, left_side=False, lower=True, transpose_a=True)
        gram_two, proj_one = lax.psum((gram_of(q_one, q_one), gram_of(q_one, b_blk)), "rows")
        low_two = jnp.linalg.cholesky(gram_two)
        proj_two = lax.linalg.triangular_solve(low_two, proj_one, left_side=True, lower=True)
        low_prod = jnp.dot(low_one, low_two, precision=HIGHEST, preferred_element_type=jnp.float32)
        x_sol = lax.linalg.triangular_solve(low_prod, proj_two, left_side=True, lower=True, transpose_a=True)
        return x_sol, low_prod.T

    row_spec = P(("batch", "rows"), None)
    out_spec = P("batch", None)
    return jax.shard_map(group_solve, mesh=mesh, in_specs=(row_spec, row_spec), out_specs=(out_spec, out_spec), check_vma=False)
```

profile of v0, /device:TPU:1, one launch (start us, length us, event | category | flops | bytes accessed | tf_op | source)
XLA Modules:
  0.0 763.1 jit_solution(8102377329612286741)
XLA Ops:
  7.2 18.4 %fusion.98 = f32[512,512]{0,1:T(8,128)} fusion(f32[4096,512]{1,0:T(8,128)} %param.3), kind=kOutput, calls=%fused_computation.172 | convolution fusion | flops 12884901888 | bytes 9437184 | tf_op jit(solution)/shard_map/dot_general | solution.py:10
  25.9 152.7 %all-reduce.5.cloned.1.call-done = f32[512,512]{0,1:T(8,128)} async-done(((f32[512,512]{0,1:T(8,128)}), f32[512,512]{0,1:T(8,128)}) %all-reduce.5.cloned.1.call-update) | async-done | bytes 1048592 | tf_op jit(solution)/shard_map/psum | solution.py:15
  183.6 11.7 %cholesky.286 = f32[128,128]{1,0:T(8,128)S(1)} custom-call(f32[128,128]{1,0:T(8,128)S(1)} %cholesky.426), custom_call_target="Cholesky" | custom-call | tf_op jit(solution)/shard_map/jit(cholesky)/cholesky | solution.py:16
  195.4 9.8 %custom-call.35 = f32[1,128,128]{1,2,0:T(8,128)S(1)} custom-call(f32[1,128,128]{2,1,0:T(8,128)S(1)} %get-tuple-element.80), custom_call_target="InvertDiagBlocksLowerTriangular" | custom-call | tf_op jit(solution)/shard_map/jit(cholesky)/cholesky | solution.py:16
  207.8 11.7 %cholesky.305 = f32[128,128]{1,0:T(8,128)S(1)} custom-call(f32[128,128]{1,0:T(8,128)S(1)} %cholesky.430), custom_call_target="Cholesky" | custom-call | tf_op jit(solution)/shard_map/jit(cholesky)/cholesky | solution.py:16
  219.6 10.2 %custom-call.36 = f32[1,128,128]{1,2,0:T(8,128)S(1)} custom-call(f32[1,128,128]{2,1,0:T(8,128)S(1)} %get-tuple-element.77), custom_call_target="InvertDiagBlocksLowerTriangular" | custom-call | tf_op jit(solution)/shard_map/jit(cholesky)/cholesky | solution.py:16
  231.4 11.7 %cholesky.326 = f32[128,128]{1,0:T(8,128)S(1)} custom-call(f32[128,128]{1,0:T(8,128)S(1)} %cholesky.435), custom_call_target="Cholesky" | custom-call | tf_op jit(solution)/shard_map/jit(cholesky)/cholesky | solution.py:16
  255.1 11.7 %cholesky.343 = f32[128,128]{1,0:T(8,128)S(1)} custom-call(f32[128,128]{1,0:T(8,128)S(1)} %convolution_subtract_fusion.13), custom_call_target="Cholesky" | custom-call | tf_op jit(solution)/shard_map/jit(cholesky)/cholesky | solution.py:16
  272.1 11.7 %while.3 = (s32[]{:T(128)}, f32[512,512]{1,0:T(8,128)}, s32[4,2]{0,1:T(2,128)S(1)}, f32[4,128,128]{2,1,0:T(8,128)S(1)}, s32[]{:T(128)}) while((s32[]{:T(128)}, f32[512,512]{1,0:T(8,128)}, s32[4,2]{0,1:T(2,128)S(1)}, f32[4,128,128]{2,1,0:T(8,128)S(1)}, s32[]{:T(128)}) %tuple.69), condition=%wide.while_cond, body=%wide.while_body.sunk | while | flops 2 | bytes 131181 | solution.py:17
  284.5 40.1 %custom-call.29 = f32[4,128,128]{1,2,0:T(8,128)S(1)} custom-call(f32[4,128,128]{2,1,0:T(8,128)} %copy-done.11), custom_call_target="InvertDiagBlocksLowerTriangular" | custom-call | tf_op jit(solution)/shard_map/triangular_solve | solution.py:17
  336.1 10.1 %convolution_subtract_fusion = f32[4096,128]{1,0:T(8,128)S(1)} fusion(f32[4096,128]{0,1:T(8,128)S(1)} %fusion.75, f32[4096,128]{0,1:T(8,128)S(1)} %bitcast.128, f32[4096,512]{1,0:T(8,128)} %param.3, f32[512,512]{1,0:T(8,128)} %get-tuple-element.233), kind=kOutput, calls=%fused_computation.13 | convolution fusion | flops 1612185600 | bytes 8519680 | tf_op jit(solution)/shard_map/triangular_solve | solution.py:17
  348.3 13.3 %fusion.8 = f32[4096,128]{1,0:T(8,128)S(1)} fusion(f32[4096,128]{0,1:T(8,128)S(1)} %fusion.74, f32[4096,128]{0,1:T(8,128)S(1)} %fusion.75, f32[4096,128]{0,1:T(8,128)S(1)} %bitcast.129, f32[4096,512]{1,0:T(8,128)} %param.3, f32[512,512]{1,0:T(8,128)} %get-tuple-element.233), kind=kOutput, calls=%fused_computation.17 | convolution fusion | flops 2419589120 | bytes 10682368 | tf_op jit(solution)/shard_map/triangular_solve | solution.py:17
  365.0 17.2 %fusion.7 = f32[512,512]{0,1:T(8,128)} fusion(f32[4096,128]{0,1:T(8,128)} %fusion.73, f32[4096,128]{0,1:T(8,128)} %copy-done.4, f32[4096,128]{0,1:T(8,128)} %copy-done.2, f32[4096,128]{0,1:T(8,128)} %bitcast.130), kind=kOutput, calls=%fused_computation.16 | convolution fusion | flops 12891193344 | bytes 9437184 | tf_op jit(solution)/shard_map/dot_general | solution.py:10
  391.9 148.7 %all-reduce.7.cloned.1.call-done = (f32[512,512]{0,1:T(8,128)}, f32[512,128]{1,0:T(8,128)}) async-done(((f32[512,512]{0,1:T(8,128)}, f32[512,128]{1,0:T(8,128)}), (f32[512,512]{0,1:T(8,128)}, f32[512,128]{1,0:T(8,128)})) %all-reduce.7.cloned.1.call-update) | async-done | bytes 1310736 | tf_op jit(solution)/shard_map/psum | solution.py:18
  545.6 11.7 %cholesky.358 = f32[128,128]{1,0:T(8,128)S(1)} custom-call(f32[128,128]{1,0:T(8,128)S(1)} %cholesky.439), custom_call_target="Cholesky" | custom-call | tf_op jit(solution)/shard_map/jit(cholesky)/cholesky | solution.py:19
  557.5 9.8 %custom-call.38 = f32[1,128,128]{1,2,0:T(8,128)S(1)} custom-call(f32[1,128,128]{2,1,0:T(8,128)S(1)} %get-tuple-element.70), custom_call_target="InvertDiagBlocksLowerTriangular" | custom-call | tf_op jit(solution)/shard_map/jit(cholesky)/cholesky | solution.py:19
  569.8 11.7 %cholesky.377 = f32[128,128]{1,0:T(8,128)S(1)} custom-call(f32[128,128]{1,0:T(8,128)S(1)} %cholesky.443), custom_call_target="Cholesky" | custom-call | tf_op jit(solution)/shard_map/jit(cholesky)/cholesky | solution.py:19
  583.0 10.2 %custom-call.39 = f32[1,128,128]{1,2,0:T(8,128)S(1)} custom-call(f32[1,128,128]{2,1,0:T(8,128)S(1)} %get-tuple-element.67), custom_call_target="InvertDiagBlocksLowerTriangular" | custom-call | tf_op jit(solution)/shard_map/jit(cholesky)/cholesky | solution.py:19
  594.7 11.7 %cholesky.398 = f32[128,128]{1,0:T(8,128)S(1)} custom-call(f32[128,128]{1,0:T(8,128)S(1)} %cholesky.448), custom_call_target="Cholesky" | custom-call | tf_op jit(solution)/shard_map/jit(cholesky)/cholesky | solution.py:19
  618.4 11.7 %cholesky.415 = f32[128,128]{1,0:T(8,128)S(1)} custom-call(f32[128,128]{1,0:T(8,128)S(1)} %convolution_subtract_fusion.12), custom_call_target="Cholesky" | custom-call | tf_op jit(solution)/shard_map/jit(cholesky)/cholesky | solution.py:19
  639.1 11.5 %while.4 = (s32[]{:T(128)}, f32[512,512]{1,0:T(8,128)}, s32[4,2]{0,1:T(2,128)S(1)}, f32[4,128,128]{2,1,0:T(8,128)S(1)}, s32[]{:T(128)}) while((s32[]{:T(128)}, f32[512,512]{1,0:T(8,128)}, s32[4,2]{0,1:T(2,128)S(1)}, f32[4,128,128]{2,1,0:T(8,128)S(1)}, s32[]{:T(128)}) %tuple.83), condition=%wide.while_cond.1, body=%wide.while_body.1.sunk | while | flops 2 | bytes 131181 | solution.py:22
  650.6 39.3 %custom-call.30 = f32[4,128,128]{1,2,0:T(8,128)S(1)} custom-call(f32[4,128,128]{2,1,0:T(8,128)S(1)} %get-tuple-element.18), custom_call_target="InvertDiagBlocksLowerTriangular" | custom-call | tf_op jit(solution)/shard_map/triangular_solve | solution.py:22
  690.0 11.2 %while.5 = (s32[]{:T(128)}, f32[512,512]{1,0:T(8,128)}, s32[4,2]{0,1:T(2,128)S(1)}, f32[4,128,128]{2,1,0:T(8,128)S(1)}, s32[]{:T(128)}) while((s32[]{:T(128)}, f32[512,512]{1,0:T(8,128)}, s32[4,2]{0,1:T(2,128)S(1)}, f32[4,128,128]{2,1,0:T(8,128)S(1)}, s32[]{:T(128)}) %tuple.84), condition=%wide.while_cond.2, body=%wide.while_body.2.sunk | while | flops 2 | bytes 131181 | solution.py:20
  701.2 39.3 %custom-call.31 = f32[4,128,128]{1,2,0:T(8,128)S(1)} custom-call(f32[4,128,128]{2,1,0:T(8,128)S(1)} %get-tuple-element.26), custom_call_target="InvertDiagBlocksLowerTriangular" | custom-call | tf_op jit(solution)/shard_map/triangular_solve | solution.py:20
  (135 shorter events, 130.3 us)
Async XLA Ops:
  7.2 375.0 %copy-start = (f32[4096,128]{1,0:T(8,128)S(1)}, f32[4096,128]{1,0:T(8,128)}, u32[]{:S(2)}) copy-start(f32[4096,128]{1,0:T(8,128)} %param.4) | copy-start | bytes 6291460
  7.2 171.4 %all-reduce.5.cloned.1.call-start = ((), (), s32[]{:S(2)}) async-start(), calls=%async_computation | async-start | bytes 2097152 | tf_op jit(solution)/shard_map/psum | solution.py:15
  25.6 514.9 %all-reduce.7.cloned.1.call-start = ((), (), s32[]{:S(2)}) async-start(), calls=%async_computation.1 | async-start | bytes 2621440 | tf_op jit(solution)/shard_map/psum | solution.py:18
  178.6 2.6 copy-start.7
  182.6 1.0 copy-start.9
  266.8 61.4 %copy-start.3 = (f32[512,512]{1,0:T(8,128)}, f32[512,512]{1,0:T(8,128)S(1)}, u32[]{:S(2)}) copy-start(f32[512,512]{1,0:T(8,128)S(1)} %get-tuple-element.72) | copy-start | bytes 3145732
  283.8 0.7 copy-start.11
  328.2 20.1 %copy-start.1 = (f32[128,4096]{1,0:T(8,128)}, f32[128,4096]{1,0:T(8,128)S(1)}, u32[]{:S(2)}) copy-start(f32[128,4096]{1,0:T(8,128)S(1)} %fusion.14) | copy-start | bytes 6291460
  336.1 12.1 %copy-start.2 = (f32[4096,128]{0,1:T(8,128)}, f32[4096,128]{0,1:T(8,128)S(1)}, u32[]{:S(2)}) copy-start(f32[4096,128]{0,1:T(8,128)S(1)} %fusion.75) | copy-start | bytes 6291460
  348.3 13.3 %copy-start.4 = (f32[4096,128]{0,1:T(8,128)}, f32[4096,128]{0,1:T(8,128)S(1)}, u32[]{:S(2)}) copy-start(f32[4096,128]{0,1:T(8,128)S(1)} %fusion.74) | copy-start | bytes 6291460
  540.6 2.6 copy-start.6
  544.6 1.0 copy-start.8
  740.5 0.7 copy-start.10
  742.3 12.5 %copy-start.5 = (f32[512,512]{1,0:T(8,128)S(1)}, f32[512,512]{1,0:T(8,128)}, u32[]{:S(2)}) copy-start(f32[512,512]{1,0:T(8,128)} %get-tuple-element.86) | copy-start | bytes 3145732
Sparse Core Ops, SparseCore 0:
  25.8 152.7 all-reduce.4
  392.0 148.4 all-reduce.6
where the time goes:
time: 768 us; the launch traced here: 763 us
  waiting for transfers between devices  301 us (39%)
  other arithmetic  283 us (37%)
  matrix products  114 us (15%)
  local copies, waits for them, and re-layouts  44.4 us (6%)
  between operations  19.8 us (3%)
    psum x1, waiting for transfers between devices, group_solve(): gram_one = lax.psum(gram_of(a_blk, a_blk), 'rows')  153 us
    psum x1, waiting for transfers between devices, group_solve(): lax.psum((gram_of(q_one, q_one), gram_of(q_one, b_blk)), 'rows')  149 us
    another operation x15, other arithmetic, group_solve(): low_two = jnp.linalg.cholesky(gram_two)  79.4 us
    another operation x14, other arithmetic, group_solve(): low_one = jnp.linalg.cholesky(gram_one)  78.9 us
    dot_general x3, matrix products, gram_of(): lax.dot_general(left_mat, right_mat, (((0,), (0,)), ((), ())), precision=...  45.3 us
    another operation x3, other arithmetic, group_solve(): lax.linalg.triangular_solve(low_one, a_blk, left_side=False, lower=True,...  41.4 us
    another operation x2, other arithmetic, group_solve(): lax.linalg.triangular_solve(low_two, proj_one, left_side=True, lower=True)  40.4 us
    another operation x7, matrix products, group_solve(): lax.linalg.triangular_solve(low_one, a_blk, left_side=False, lower=True,...  40.2 us
  transfers between devices with their start and end apart: 2, of which 2 were waited for; matrix products, arithmetic and copies ran while one was open for 0% of the time, Pallas kernels for 0%

commit v1 on v0

v1 whole, which is shorter than its diff:
```python
import functools
import jax, jax.numpy as jnp
from jax import lax
from jax.experimental import pallas as pl
from jax.experimental.pallas import tpu as pltpu
from jax.sharding import PartitionSpec as P

HIGHEST = lax.Precision.HIGHEST
CHIPS = 64
CH = 16


def owner_index(chip, n_own):
    idx = (chip * n_own + CHIPS - 1) // CHIPS
    return idx, jnp.logical_and((idx * CHIPS) // n_own == chip, idx < n_own)


def sum_kernel(n_own, x_ref, o_ref, pair_buf, part, rs_buf, red, sems):
    dev = lax.axis_index("rows")
    chip, core = dev // 2, dev % 2
    half = n_own * CH
    mine = pl.multiple_of(core * half, CH)
    other = pl.multiple_of((1 - core) * half, CH)
    partner = {"rows": chip * 2 + 1 - core}

    def peer(step):
        t = (chip + step) % CHIPS
        return t, {"rows": t * 2 + core}

    barrier = pltpu.get_barrier_semaphore()
    pl.semaphore_signal(barrier, inc=1, device_id=partner)

    @pl.loop(1, CHIPS)
    def _(step):
        pl.semaphore_signal(barrier, inc=1, device_id=peer(step)[1])
    pl.semaphore_wait(barrier, CHIPS)

    pair = pltpu.make_async_remote_copy(x_ref.at[pl.ds(other, half)], pair_buf, sems.at[0], sems.at[1], device_id=partner)
    pair.start()
    pair.wait()
    part[...] = x_ref[pl.ds(mine, half), :] + pair_buf[...]

    my_idx, owner = owner_index(chip, n_own)
    my_row = pl.multiple_of(my_idx * CH, CH)

    @pl.loop(1, CHIPS)
    def _(step):
        t, dst = peer(step)
        idx, owns = owner_index(t, n_own)

        @pl.when(owns)
        def _():
            pltpu.make_async_remote_copy(part.at[pl.ds(pl.multiple_of(idx * CH, CH), CH)],
                                         rs_buf.at[pl.ds(pl.multiple_of((step - 1) * CH, CH), CH)],
                                         sems.at[2], sems.at[3], device_id=dst).start()

    def wait_rows(n, sem):
        pltpu.make_async_copy(part.at[pl.ds(0, n * CH)], part.at[pl.ds(0, n * CH)], sem).wait()

    @pl.when(owner)
    def _():
        pltpu.make_async_copy(rs_buf, rs_buf, sems.at[3]).wait()
        tot = part[pl.ds(my_row, CH), :]
        for s in range(CHIPS - 1):
            tot = tot + rs_buf[pl.ds(s * CH, CH), :]
        red[...] = tot
        o_ref[pl.ds(mine + my_row, CH), :] = tot

        @pl.loop(1, CHIPS)
        def _(step):
            pltpu.make_async_remote_copy(red, o_ref.at[pl.ds(pl.multiple_of(mine + my_row, CH), CH)],
                                         sems.at[4], sems.at[5], device_id=peer(step)[1]).start()
        wait_rows(n_own - 1, sems.at[2])
        wait_rows(n_own - 1, sems.at[5])

    @pl.when(jnp.logical_not(owner))
    def _():
        wait_rows(n_own, sems.at[2])
        wait_rows(n_own, sems.at[5])

    swap = pltpu.make_async_remote_copy(o_ref.at[pl.ds(mine, half)], o_ref.at[pl.ds(mine, half)], sems.at[6], sems.at[7], device_id=partner)
    swap.start()
    swap.wait()

    @pl.when(owner)
    def _():
        pltpu.make_async_copy(rs_buf, rs_buf, sems.at[4]).wait()


def sum_all(x, cid):
    rows = x.shape[0]
    half = rows // 2
    n_own = half // CH
    return pl.pallas_call(
        functools.partial(sum_kernel, n_own),
        out_shape=jax.ShapeDtypeStruct(x.shape, jnp.float32),
        in_specs=[pl.BlockSpec(memory_space=pltpu.VMEM)],
        out_specs=pl.BlockSpec(memory_space=pltpu.VMEM),
        scratch_shapes=[pltpu.VMEM((half, 128), jnp.float32), pltpu.VMEM((half, 128), jnp.float32),
                        pltpu.VMEM(((CHIPS - 1) * CH, 128), jnp.float32), pltpu.VMEM((CH, 128), jnp.float32),
                        pltpu.SemaphoreType.DMA((8,))],
        compiler_params=pltpu.CompilerParams(collective_id=cid, has_side_effects=True),
        name="sum_rows",
    )(x)


def gram_of(left_mat, right_mat):
    return lax.dot_general(left_mat, right_mat, (((0,), (0,)), ((), ())), precision=HIGHEST, preferred_element_type=jnp.float32)


TILES = [(i, j) for i in range(4) for j in range(i + 1)]


def pack(gram):
    return jnp.concatenate([gram[i * 128:(i + 1) * 128, j * 128:(j + 1) * 128] for i, j in TILES], axis=0)


def unpack(tiles):
    blk = {ij: tiles[k * 128:(k + 1) * 128] for k, ij in enumerate(TILES)}
    return jnp.concatenate([jnp.concatenate([blk[i, j] if i >= j else blk[j, i].T for j in range(4)], axis=1) for i in range(4)], axis=0)


def solution(mesh):
    def group_solve(a_blk, b_blk):
        gram_one = unpack(sum_all(pack(gram_of(a_blk, a_blk)), 0))
        low_one = jnp.linalg.cholesky(gram_one)
        q_one = lax.linalg.triangular_solve(low_one, a_blk, left_side=False, lower=True, transpose_a=True)
        both = sum_all(jnp.concatenate([pack(gram_of(q_one, q_one)), gram_of(q_one, b_blk)], axis=0), 1)
        gram_two, proj_one = unpack(both[:1280]), both[1280:]
        low_two = jnp.linalg.cholesky(gram_two)
        proj_two = lax.linalg.triangular_solve(low_two, proj_one, left_side=True, lower=True)
        low_prod = jnp.dot(low_one, low_two, precision=HIGHEST, preferred_element_type=jnp.float32)
        x_sol = lax.linalg.triangular_solve(low_prod, proj_two, left_side=True, lower=True, transpose_a=True)
        return x_sol, low_prod.T

    row_spec = P(("batch", "rows"), None)
    out_spec = P("batch", None)
    return jax.shard_map(group_solve, mesh=mesh, in_specs=(row_spec, row_spec), out_specs=(out_spec, out_spec), check_vma=False)
```

time: 768 us -> 558 us (0.73)
  waiting for transfers between devices: 301 us -> 0 us
  Pallas kernels: 0 us -> 62.3 us
  local copies, waits for them, and re-layouts: 44.4 us -> 74.6 us
  between operations: 19.8 us -> 6.89 us
  other arithmetic: 283 us -> 293 us
    psum x2 -> x0, waiting for transfers between devices: 301 us -> none  [the longest x1 153 us: group_solve(): gram_one = lax.psum(gram_of(a_blk, a_blk), 'rows')]
    pallas_call x0 -> x2, Pallas kernels: none -> 62.3 us  [sum_all(): pl.pallas_call(functools.partial(sum_kernel, n_own), out_shape=jax.ShapeD...]
    unnamed x28 -> x69, local copies, waits for them, and re-layouts: 4.72 us -> 26.2 us
    another operation x14 -> x15, other arithmetic: 78.9 us -> 79.6 us  [group_solve(): low_one = jnp.linalg.cholesky(gram_one)]
  transfers between devices with their start and end apart: 2 -> 0, of which waited for: 2 -> 0; matrix products, arithmetic and copies ran while one was open for 0% -> 0% of each run, Pallas kernels for 0% -> 0%
where the time goes in v1:
time: 558 us; the launch traced here: 552 us
  other arithmetic  293 us (53%)
  matrix products  115 us (21%)
  local copies, waits for them, and re-layouts  74.6 us (13%)
  Pallas kernels  62.3 us (11%)
  between operations  6.89 us (1%)
    another operation x15, other arithmetic, group_solve(): low_two = jnp.linalg.cholesky(gram_two)  81.4 us
    another operation x15, other arithmetic, group_solve(): low_one = jnp.linalg.cholesky(gram_one)  79.6 us
    pallas_call x2, Pallas kernels, sum_all(): pl.pallas_call(functools.partial(sum_kernel, n_own), out_shape=jax.ShapeD...  62.3 us
    dot_general x3, matrix products, gram_of(): lax.dot_general(left_mat, right_mat, (((0,), (0,)), ((), ())), precision=...  44.2 us
    another operation x2, other arithmetic, group_solve(): lax.linalg.triangular_solve(low_two, proj_one, left_side=True, lower=True)  42.1 us
    another operation x3, other arithmetic, group_solve(): lax.linalg.triangular_solve(low_one, a_blk, left_side=False, lower=True,...  41.2 us
    another operation x7, matrix products, group_solve(): lax.linalg.triangular_solve(low_one, a_blk, left_side=False, lower=True,...  40.2 us
    another operation x2, other arithmetic, group_solve(): lax.linalg.triangular_solve(low_prod, proj_two, left_side=True, lower=Tru...  40 us

profile of v1, /device:TPU:1, one launch (start us, length us, event | category | flops | bytes accessed | tf_op | source)
XLA Modules:
  0.0 551.6 jit_solution(17550034466913416710)
XLA Ops:
  0.6 17.3 %fusion.101 = f32[512,512]{1,0:T(8,128)S(1)} fusion(f32[4096,512]{1,0:T(8,128)} %param.3), kind=kOutput, calls=%fused_computation.203 | convolution fusion | flops 12884901888 | bytes 9437184 | tf_op jit(solution)/shard_map/dot_general | solution.py:108
  19.0 31.2 %sum_rows.2 = f32[1280,128]{1,0:T(8,128)} custom-call(f32[1280,128]{1,0:T(8,128)} %copy-done.10), custom_call_target="tpu_custom_call" | custom-call | tf_op jit(solution)/shard_map/sum_rows/pallas_call | solution.py:94
  60.3 11.7 %cholesky.286 = f32[128,128]{1,0:T(8,128)S(1)} custom-call(f32[128,128]{1,0:T(8,128)S(1)} %cholesky.426), custom_call_target="Cholesky" | custom-call | tf_op jit(solution)/shard_map/jit(cholesky)/cholesky | solution.py:126
  72.2 9.8 %custom-call.35 = f32[1,128,128]{1,2,0:T(8,128)S(1)} custom-call(f32[1,128,128]{2,1,0:T(8,128)S(1)} %get-tuple-element.102), custom_call_target="InvertDiagBlocksLowerTriangular" | custom-call | tf_op jit(solution)/shard_map/jit(cholesky)/cholesky | solution.py:126
  84.5 11.7 %cholesky.305 = f32[128,128]{1,0:T(8,128)S(1)} custom-call(f32[128,128]{1,0:T(8,128)S(1)} %cholesky.430), custom_call_target="Cholesky" | custom-call | tf_op jit(solution)/shard_map/jit(cholesky)/cholesky | solution.py:126
  98.9 10.2 %custom-call.36 = f32[1,128,128]{1,2,0:T(8,128)S(1)} custom-call(f32[1,128,128]{2,1,0:T(8,128)S(1)} %get-tuple-element.99), custom_call_target="InvertDiagBlocksLowerTriangular" | custom-call | tf_op jit(solution)/shard_map/jit(cholesky)/cholesky | solution.py:126
  110.7 11.7 %cholesky.326 = f32[128,128]{1,0:T(8,128)S(1)} custom-call(f32[128,128]{1,0:T(8,128)S(1)} %cholesky.435), custom_call_target="Cholesky" | custom-call | tf_op jit(solution)/shard_map/jit(cholesky)/cholesky | solution.py:126
  123.8 9.8 %custom-call.37 = f32[1,128,128]{1,2,0:T(8,128)S(1)} custom-call(f32[1,128,128]{2,1,0:T(8,128)S(1)} %get-tuple-element.96), custom_call_target="InvertDiagBlocksLowerTriangular" | custom-call | tf_op jit(solution)/shard_map/jit(cholesky)/cholesky | solution.py:126
  135.0 11.9 %cholesky.343 = f32[128,128]{1,0:T(8,128)S(1)} custom-call(f32[128,128]{1,0:T(8,128)S(1)} %convolution_subtract_fusion.13), custom_call_target="Cholesky" | custom-call | tf_op jit(solution)/shard_map/jit(cholesky)/cholesky | solution.py:126
  149.3 11.7 %while.3 = (s32[]{:T(128)}, f32[512,512]{1,0:T(8,128)}, s32[4,2]{0,1:T(2,128)S(1)}, f32[4,128,128]{2,1,0:T(8,128)S(1)}, s32[]{:T(128)}) while((s32[]{:T(128)}, f32[512,512]{1,0:T(8,128)}, s32[4,2]{0,1:T(2,128)S(1)}, f32[4,128,128]{2,1,0:T(8,128)S(1)}, s32[]{:T(128)}) %tuple.91), condition=%wide.while_cond, body=%wide.while_body.sunk | while | flops 2 | bytes 131181 | solution.py:127
  161.8 40.1 %custom-call.29 = f32[4,128,128]{1,2,0:T(8,128)S(1)} custom-call(f32[4,128,128]{2,1,0:T(8,128)} %copy-done.17), custom_call_target="InvertDiagBlocksLowerTriangular" | custom-call | tf_op jit(solution)/shard_map/triangular_solve | solution.py:127
  213.4 10.1 %convolution_subtract_fusion = f32[4096,128]{1,0:T(8,128)S(1)} fusion(f32[4096,128]{0,1:T(8,128)S(1)} %fusion.75, f32[4096,128]{0,1:T(8,128)S(1)} %bitcast.144, f32[4096,512]{1,0:T(8,128)} %param.3, f32[512,512]{1,0:T(8,128)} %get-tuple-element.245), kind=kOutput, calls=%fused_computation.13 | convolution fusion | flops 1612185600 | bytes 8519680 | tf_op jit(solution)/shard_map/triangular_solve | solution.py:127
  225.5 13.3 %fusion.8 = f32[4096,128]{1,0:T(8,128)S(1)} fusion(f32[4096,128]{0,1:T(8,128)S(1)} %fusion.74, f32[4096,128]{0,1:T(8,128)S(1)} %fusion.75, f32[4096,128]{0,1:T(8,128)S(1)} %bitcast.145, f32[4096,512]{1,0:T(8,128)} %param.3, f32[512,512]{1,0:T(8,128)} %get-tuple-element.245), kind=kOutput, calls=%fused_computation.17 | convolution fusion | flops 2419589120 | bytes 10682368 | tf_op jit(solution)/shard_map/triangular_solve | solution.py:127
  242.2 17.3 %fusion.7 = f32[512,512]{1,0:T(8,128)} fusion(f32[4096,128]{0,1:T(8,128)} %fusion.73, f32[4096,128]{0,1:T(8,128)} %copy-done.3, f32[4096,128]{0,1:T(8,128)} %copy-done.2, f32[4096,128]{0,1:T(8,128)} %bitcast.146), kind=kOutput, calls=%fused_computation.16 | convolution fusion | flops 12891193344 | bytes 9437184 | tf_op jit(solution)/shard_map/dot_general | solution.py:108
  282.3 31.1 %sum_rows.3 = f32[1792,128]{1,0:T(8,128)} custom-call(f32[1792,128]{1,0:T(8,128)} %fusion.16.x_ref), custom_call_target="tpu_custom_call" | custom-call | tf_op jit(solution)/shard_map/sum_rows/pallas_call | solution.py:94
  334.6 11.7 %cholesky.358 = f32[128,128]{1,0:T(8,128)S(1)} custom-call(f32[128,128]{1,0:T(8,128)S(1)} %cholesky.439), custom_call_target="Cholesky" | custom-call | tf_op jit(solution)/shard_map/jit(cholesky)/cholesky | solution.py:130
  360.5 11.7 %cholesky.377 = f32[128,128]{1,0:T(8,128)S(1)} custom-call(f32[128,128]{1,0:T(8,128)S(1)} %cholesky.443), custom_call_target="Cholesky" | custom-call | tf_op jit(solution)/shard_map/jit(cholesky)/cholesky | solution.py:130
  375.5 10.2 %custom-call.39 = f32[1,128,128]{1,2,0:T(8,128)S(1)} custom-call(f32[1,128,128]{2,1,0:T(8,128)S(1)} %get-tuple-element.89), custom_call_target="InvertDiagBlocksLowerTriangular" | custom-call | tf_op jit(solution)/shard_map/jit(cholesky)/cholesky | solution.py:130
  388.0 11.7 %cholesky.398 = f32[128,128]{1,0:T(8,128)S(1)} custom-call(f32[128,128]{1,0:T(8,128)S(1)} %cholesky.448), custom_call_target="Cholesky" | custom-call | tf_op jit(solution)/shard_map/jit(cholesky)/cholesky | solution.py:130
  413.8 11.9 %cholesky.415 = f32[128,128]{1,0:T(8,128)S(1)} custom-call(f32[128,128]{1,0:T(8,128)S(1)} %convolution_subtract_fusion.12), custom_call_target="Cholesky" | custom-call | tf_op jit(solution)/shard_map/jit(cholesky)/cholesky | solution.py:130
  432.1 11.6 %while.4 = (s32[]{:T(128)}, f32[512,512]{1,0:T(8,128)}, s32[4,2]{0,1:T(2,128)S(1)}, f32[4,128,128]{2,1,0:T(8,128)S(1)}, s32[]{:T(128)}) while((s32[]{:T(128)}, f32[512,512]{1,0:T(8,128)}, s32[4,2]{0,1:T(2,128)S(1)}, f32[4,128,128]{2,1,0:T(8,128)S(1)}, s32[]{:T(128)}) %tuple.100), condition=%wide.while_cond.1, body=%wide.while_body.1.sunk | while | flops 2 | bytes 131181 | solution.py:133
  443.7 39.3 %custom-call.30 = f32[4,128,128]{1,2,0:T(8,128)S(1)} custom-call(f32[4,128,128]{2,1,0:T(8,128)S(1)} %get-tuple-element.18), custom_call_target="InvertDiagBlocksLowerTriangular" | custom-call | tf_op jit(solution)/shard_map/triangular_solve | solution.py:133
  485.1 10.6 %while.5 = (s32[]{:T(128)}, f32[512,512]{1,0:T(8,128)S(1)}, s32[4,2]{0,1:T(2,128)S(1)}, f32[4,128,128]{2,1,0:T(8,128)}, s32[]{:T(128)}) while((s32[]{:T(128)}, f32[512,512]{1,0:T(8,128)S(1)}, s32[4,2]{0,1:T(2,128)S(1)}, f32[4,128,128]{2,1,0:T(8,128)}, s32[]{:T(128)}) %tuple.101), condition=%wide.while_cond.2, body=%wide.while_body.2.sunk | while | flops 2 | bytes 132705 | solution.py:131
  495.7 40.8 %custom-call.31 = f32[4,128,128]{1,2,0:T(8,128)} custom-call(f32[4,128,128]{2,1,0:T(8,128)} %get-tuple-element.26), custom_call_target="InvertDiagBlocksLowerTriangular" | custom-call | tf_op jit(solution)/shard_map/triangular_solve | solution.py:131
  (187 shorter events, 170.0 us)
Async XLA Ops:
  0.6 272.2 %copy-start = (f32[4096,128]{1,0:T(8,128)S(1)}, f32[4096,128]{1,0:T(8,128)}, u32[]{:S(2)}) copy-start(f32[4096,128]{1,0:T(8,128)} %param.4) | copy-start | bytes 6291460
  18.2 0.8 copy-start.10
  52.1 2.8 copy-start.11
  52.1 2.8 copy-start.12
  52.4 2.5 copy-start.9
  52.8 2.1 copy-start.8
  53.8 1.1 copy-start.13
  54.7 0.6 copy-start.14
  54.8 0.6 copy-start.15
  59.3 1.0 copy-start.6
  161.1 0.7 copy-start.17
  205.4 20.1 %copy-start.1 = (f32[128,4096]{1,0:T(8,128)}, f32[128,4096]{1,0:T(8,128)S(1)}, u32[]{:S(2)}) copy-start(f32[128,4096]{1,0:T(8,128)S(1)} %fusion.14) | copy-start | bytes 6291460
  213.4 12.1 %copy-start.2 = (f32[4096,128]{0,1:T(8,128)}, f32[4096,128]{0,1:T(8,128)S(1)}, u32[]{:S(2)}) copy-start(f32[4096,128]{0,1:T(8,128)S(1)} %fusion.75) | copy-start | bytes 6291460
  225.5 13.3 %copy-start.3 = (f32[4096,128]{0,1:T(8,128)}, f32[4096,128]{0,1:T(8,128)S(1)}, u32[]{:S(2)}) copy-start(f32[4096,128]{0,1:T(8,128)S(1)} %fusion.74) | copy-start | bytes 6291460
  315.3 0.6 copy-start.16
  333.6 1.0 copy-start.7
  495.7 40.8 %copy-start.5 = (f32[512,512]{1,0:T(8,128)}, f32[512,512]{1,0:T(8,128)S(1)}, u32[]{:S(2)}) copy-start(f32[512,512]{1,0:T(8,128)S(1)} %get-tuple-element.244) | copy-start | bytes 3145732
  537.6 12.5 %copy-start.4 = (f32[512,512]{1,0:T(8,128)S(1)}, f32[512,512]{1,0:T(8,128)}, u32[]{:S(2)}) copy-start(f32[512,512]{1,0:T(8,128)} %get-tuple-element.108) | copy-start | bytes 3145732

commit v2 on v1

--- a/solution.py
+++ b/solution.py
@@ -104,34 +104,207 @@
     )(x)
 
 
-def gram_of(left_mat, right_mat):
-    return lax.dot_general(left_mat, right_mat, (((0,), (0,)), ((), ())), precision=HIGHEST, preferred_element_type=jnp.float32)
-
-
-TILES = [(i, j) for i in range(4) for j in range(i + 1)]
-
-
-def pack(gram):
-    return jnp.concatenate([gram[i * 128:(i + 1) * 128, j * 128:(j + 1) * 128] for i, j in TILES], axis=0)
-
-
-def unpack(tiles):
-    blk = {ij: tiles[k * 128:(k + 1) * 128] for k, ij in enumerate(TILES)}
-    return jnp.concatenate([jnp.concatenate([blk[i, j] if i >= j else blk[j, i].T for j in range(4)], axis=1) for i in range(4)], axis=0)
+TRI = [(j, i) for j in range(4) for i in range(j, 4)]
+TILE = 512
+GIVE = 60 * 1024 * 1024
+
+
+def mm(a, b):
+    return lax.dot_general(a, b, (((1,), (0,)), ((), ())), precision=HIGHEST, preferred_element_type=jnp.float32)
+
+
+def mm_t(a, b):
+    return lax.dot_general(a, b, (((0,), (0,)), ((), ())), precision=HIGHEST, preferred_element_type=jnp.float32)
+
+
+def pack_into(o_ref, g_ref):
+    for t, (j, i) in enumerate(TRI):
+        o_ref[t * 128:t * 128 + 128, :] = g_ref[j * 128:j * 128 + 128, i * 128:i * 128 + 128]
+
+
+def gram_kernel(a_ref, o_ref, acc):
+    step = pl.program_id(0)
+
+    @pl.when(step == 0)
+    def _():
+        acc[...] = jnp.zeros_like(acc)
+    acc[:256, :] += mm_t(a_ref[:, :256], a_ref[...])
+    acc[256:, 256:] += mm_t(a_ref[:, 256:], a_ref[:, 256:])
+
+    @pl.when(step == pl.num_programs(0) - 1)
+    def _():
+        pack_into(o_ref, acc)
+
+
+def local_gram(a_blk):
+    rows = a_blk.shape[0]
+    return pl.pallas_call(
+        gram_kernel, grid=(rows // TILE,),
+        out_shape=jax.ShapeDtypeStruct((1280, 128), jnp.float32),
+        in_specs=[pl.BlockSpec((TILE, 512), lambda i: (i, 0))],
+        out_specs=pl.BlockSpec((1280, 128), lambda i: (0, 0)),
+        scratch_shapes=[pltpu.VMEM((512, 512), jnp.float32)],
+        compiler_params=pltpu.CompilerParams(dimension_semantics=("arbitrary",), vmem_limit_bytes=GIVE),
+        name="gram_one",
+    )(a_blk)
+
+
+def second_kernel(a_ref, b_ref, r_ref, x_ref, o_ref, acc, proj):
+    step = pl.program_id(0)
+
+    @pl.when(step == 0)
+    def _():
+        acc[...] = jnp.zeros_like(acc)
+        proj[...] = jnp.zeros_like(proj)
+    q_lo = mm(a_ref[:, :256], x_ref[:256, :])
+    q_hi = mm(a_ref[:, 256:] - mm(q_lo, r_ref[:256, 256:]), x_ref[256:, :])
+    b_blk = b_ref[...]
+    acc[:256, :256] += mm_t(q_lo, q_lo)
+    acc[:256, 256:] += mm_t(q_lo, q_hi)
+    acc[256:, 256:] += mm_t(q_hi, q_hi)
+    proj[:256, :] += mm_t(q_lo, b_blk)
+    proj[256:, :] += mm_t(q_hi, b_blk)
+
+    @pl.when(step == pl.num_programs(0) - 1)
+    def _():
+        pack_into(o_ref, acc)
+        o_ref[1280:, :] = proj[...]
+
+
+def second_pass(a_blk, b_blk, r_one, x_one):
+    rows = a_blk.shape[0]
+    return pl.pallas_call(
+        second_kernel, grid=(rows // TILE,),
+        out_shape=jax.ShapeDtypeStruct((1792, 128), jnp.float32),
+        in_specs=[pl.BlockSpec((TILE, 512), lambda i: (i, 0)), pl.BlockSpec((TILE, 128), lambda i: (i, 0)),
+                  pl.BlockSpec((512, 512), lambda i: (0, 0)), pl.BlockSpec((512, 256), lambda i: (0, 0))],
+        out_specs=pl.BlockSpec((1792, 128), lambda i: (0, 0)),
+        scratch_shapes=[pltpu.VMEM((512, 512), jnp.float32), pltpu.VMEM((512, 128), jnp.float32)],
+        compiler_params=pltpu.CompilerParams(dimension_semantics=("arbitrary",), vmem_limit_bytes=GIVE),
+        name="second_pass",
+    )(a_blk, b_blk, r_one, x_one)
+
+
+def factor_block(d_mat):
+    sub = lax.broadcasted_iota(jnp.int32, (8, 128), 0)
+    lane = lax.broadcasted_iota(jnp.int32, (8, 128), 1)
+    d_row = lax.broadcasted_iota(jnp.int32, (128, 128), 0)
+    d_col = lax.broadcasted_iota(jnp.int32, (128, 128), 1)
+    d_mat = jnp.where(d_col >= d_row, d_mat, d_mat.T)
+    rows = [d_mat[8 * i:8 * i + 8, :] for i in range(16)]
+    inv = [jnp.where(lane == sub + 8 * i, 1.0, 0.0).astype(jnp.float32) for i in range(16)]
+    r_out, v_out = [], []
+    for k in range(16):
+        cols = {i: [jnp.broadcast_to(rows[i][:, 8 * k + r:8 * k + r + 1], (8, 128)) for r in range(8)] for i in range(k, 16)}
+        scale = jnp.zeros((8, 128), jnp.float32)
+        top = cols[k]
+        for r in range(8):
+            inv_root = lax.rsqrt(jnp.broadcast_to(top[r][r:r + 1, :], (8, 128)))
+            scale = jnp.where(sub == r, inv_root, scale)
+            below = jnp.where(sub > r, top[r] * inv_root, 0.0)
+            row_s = jnp.broadcast_to(rows[k][r:r + 1, :], (8, 128)) * inv_root
+            row_v = jnp.broadcast_to(inv[k][r:r + 1, :], (8, 128)) * inv_root
+            coef = [jnp.broadcast_to(top[c][r:r + 1, :], (8, 128)) * inv_root for c in range(r + 1, 8)]
+            for c in range(r + 1, 8):
+                top[c] = top[c] - below * coef[c - r - 1]
+            rows[k] = rows[k] - below * row_s
+            inv[k] = inv[k] - below * row_v
+            for i in range(k + 1, 16):
+                mult = cols[i][r] * inv_root
+                for c in range(r + 1, 8):
+                    cols[i][c] = cols[i][c] - mult * coef[c - r - 1]
+                rows[i] = rows[i] - mult * row_s
+                inv[i] = inv[i] - mult * row_v
+        r_out.append(jnp.where(lane >= sub + 8 * k, rows[k] * scale, 0.0))
+        v_out.append(inv[k] * scale)
+    return r_out, v_out
+
+
+def factor(g_ref, r_out, x_out, s_mat, v_mat, r_mat):
+    width = s_mat.shape[1]
+    for t, (j, i) in enumerate(TRI):
+        s_mat[j * 128:j * 128 + 128, i * 128:i * 128 + 128] = g_ref[t * 128:t * 128 + 128, :]
+    if width > 512:
+        s_mat[:, 512:] = g_ref[1280:, :]
+
+    @pl.loop(0, 4)
+    def _(j):
+        top = pl.multiple_of(j * 128, 128)
+        r_blk, v_blk = factor_block(s_mat[pl.ds(top, 128), pl.ds(top, 128)])
+        for i in range(16):
+            r_mat[pl.ds(top + 8 * i, 8), pl.ds(top, 128)] = r_blk[i]
+            v_mat[pl.ds(top + 8 * i, 8), :] = v_blk[i]
+        for jj in range(4):
+            lo, hi = 128 * jj, 128 * jj + 128
+            if hi < width:
+                @pl.when(j == jj)
+                def _():
+                    row = mm(v_mat[lo:hi, :], s_mat[lo:hi, hi:])
+                    r_mat[lo:hi, hi:] = row
+                    if hi < 512:
+                        s_mat[hi:, hi:] = s_mat[hi:, hi:] - mm_t(row[:, :512 - hi], row)
+    for jj in range(1, 4):
+        r_mat[128 * jj:128 * jj + 128, :128 * jj] = jnp.zeros((128, 128 * jj), jnp.float32)
+    for p in range(2):
+        lo, mid, hi = 256 * p, 256 * p + 128, 256 * p + 256
+        x_lo, x_hi = v_mat[lo:mid, :].T, v_mat[mid:hi, :].T
+        x_out[lo:mid, :128] = x_lo
+        x_out[mid:hi, 128:] = x_hi
+        x_out[mid:hi, :128] = jnp.zeros((128, 128), jnp.float32)
+        x_out[lo:mid, 128:] = -mm(x_lo, mm(r_mat[lo:mid, mid:hi], x_hi))
+
+
+def chol_kernel(g_ref, r_out, x_out, s_mat, v_mat):
+    factor(g_ref, r_out, x_out, s_mat, v_mat, r_out)
+
+
+def chol_one(tiles):
+    return pl.pallas_call(
+        chol_kernel,
+        out_shape=(jax.ShapeDtypeStruct((512, 512), jnp.float32), jax.ShapeDtypeStruct((512, 256), jnp.float32)),
+        in_specs=[pl.BlockSpec(memory_space=pltpu.VMEM)],
+        out_specs=(pl.BlockSpec(memory_space=pltpu.VMEM),) * 2,
+        scratch_shapes=[pltpu.VMEM((512, 512), jnp.float32), pltpu.VMEM((512, 128), jnp.float32)],
+        compiler_params=pltpu.CompilerParams(vmem_limit_bytes=GIVE),
+        name="chol_one",
+    )(tiles)
+
+
+def back_solve(r_ref, x_ref, y_lo, y_hi):
+    z_hi = mm(x_ref[256:, :], y_hi)
+    z_lo = mm(x_ref[:256, :], y_lo - mm(r_ref[:256, 256:512], z_hi))
+    return z_lo, z_hi
+
+
+def last_kernel(g_ref, r_one, x_one, sol, r_fac, s_mat, v_mat, r_two, x_two):
+    factor(g_ref, r_two, x_two, s_mat, v_mat, r_two)
+    z_lo, z_hi = back_solve(r_two, x_two, r_two[:256, 512:], r_two[256:, 512:])
+    s_lo, s_hi = back_solve(r_one, x_one, z_lo, z_hi)
+    sol[:256, :] = s_lo
+    sol[256:, :] = s_hi
+    r_fac[:256, :256] = mm(r_two[:256, :256], r_one[:256, :256])
+    r_fac[:256, 256:] = mm(r_two[:256, :512], r_one[:, 256:])
+    r_fac[256:, 256:] = mm(r_two[256:, 256:512], r_one[256:, 256:])
+    r_fac[256:, :256] = jnp.zeros((256, 256), jnp.float32)
+
+
+def finish(tiles, r_one, x_one):
+    return pl.pallas_call(
+        last_kernel,
+        out_shape=(jax.ShapeDtypeStruct((512, 128), jnp.float32), jax.ShapeDtypeStruct((512, 512), jnp.float32)),
+        in_specs=[pl.BlockSpec(memory_space=pltpu.VMEM)] * 3,
+        out_specs=(pl.BlockSpec(memory_space=pltpu.VMEM),) * 2,
+        scratch_shapes=[pltpu.VMEM((512, 640), jnp.float32), pltpu.VMEM((512, 128), jnp.float32),
+                        pltpu.VMEM((512, 640), jnp.float32), pltpu.VMEM((512, 256), jnp.float32)],
+        compiler_params=pltpu.CompilerParams(vmem_limit_bytes=GIVE),
+        name="finish",
+    )(tiles, r_one, x_one)
 
 
 def solution(mesh):
     def group_solve(a_blk, b_blk):
-        gram_one = unpack(sum_all(pack(gram_of(a_blk, a_blk)), 0))
-        low_one = jnp.linalg.cholesky(gram_one)
-        q_one = lax.linalg.triangular_solve(low_one, a_blk, left_side=False, lower=True, transpose_a=True)
-        both = sum_all(jnp.concatenate([pack(gram_of(q_one, q_one)), gram_of(q_one, b_blk)], axis=0), 1)
-        gram_two, proj_one = unpack(both[:1280]), both[1280:]
-        low_two = jnp.linalg.cholesky(gram_two)
-        proj_two = lax.linalg.triangular_solve(low_two, proj_one, left_side=True, lower=True)
-        low_prod = jnp.dot(low_one, low_two, precision=HIGHEST, preferred_element_type=jnp.float32)
-        x_sol = lax.linalg.triangular_solve(low_prod, proj_two, left_side=True, lower=True, transpose_a=True)
-        return x_sol, low_prod.T
+        r_one, x_one = chol_one(sum_all(local_gram(a_blk), 0))
+        return finish(sum_all(second_pass(a_blk, b_blk, r_one, x_one), 1), r_one, x_one)
 
     row_spec = P(("batch", "rows"), None)
     out_spec = P("batch", None)

time: 558 us -> 163 us (0.29); the launches traced: 552 us -> 163 us
  other arithmetic: 293 us -> 0 us
  matrix products: 115 us -> 0 us
  Pallas kernels: 62.3 us -> 162 us
  local copies, waits for them, and re-layouts: 74.6 us -> 0 us
  between operations: 6.89 us -> 0.65 us
    another operation x37 -> x0, other arithmetic: 284 us -> none  [the longest x15 81.4 us: group_solve(): low_two = jnp.linalg.cholesky(gram_two)]
    pallas_call x0 -> x4, Pallas kernels: none -> 100 us  [the longest x1 37.9 us: second_pass(): pl.pallas_call(second_kernel, grid=(rows // TILE,), out_shape=jax.ShapeDt...]
    another operation x33 -> x0, matrix products: 66.2 us -> none  [the longest x7 40.2 us: group_solve(): lax.linalg.triangular_solve(low_one, a_blk, left_side=False, lower=True,...]
    dot_general x4 -> x0, matrix products: 48.7 us -> none  [the longest x3 44.2 us: gram_of(): lax.dot_general(left_mat, right_mat, (((0,), (0,)), ((), ())), precision=...]
    another operation x45 -> x0, local copies, waits for them, and re-layouts: 35 us -> none
    unnamed x69 -> x0, local copies, waits for them, and re-layouts: 26.2 us -> none
    concatenate x7 -> x0, local copies, waits for them, and re-layouts: 7.23 us -> none  [the longest x2 4.1 us: unpack(): jnp.concatenate([jnp.concatenate([blk[i, j] if i >= j else blk[j, i].T fo...]
    slice x4 -> x0, local copies, waits for them, and re-layouts: 6.27 us -> none  [unpack(): blk = {ij: tiles[k * 128:(k + 1) * 128] for k, ij in enumerate(TILES)}]
where the time goes in v2:
time: 163 us
  Pallas kernels  162 us (99%)
    pallas_call x2, Pallas kernels, sum_all(): pl.pallas_call(functools.partial(sum_kernel, n_own), out_shape=jax.ShapeD...  62.1 us
    pallas_call x1, Pallas kernels, second_pass(): pl.pallas_call(second_kernel, grid=(rows // TILE,), out_shape=jax.ShapeDt...  37.9 us
    pallas_call x1, Pallas kernels, finish(): pl.pallas_call(last_kernel, out_shape=(jax.ShapeDtypeStruct((512, 128), j...  26 us
    pallas_call x1, Pallas kernels, chol_one(): pl.pallas_call(chol_kernel, out_shape=(jax.ShapeDtypeStruct((512, 512), j...  21.6 us
    pallas_call x1, Pallas kernels, local_gram(): pl.pallas_call(gram_kernel, grid=(rows // TILE,), out_shape=jax.ShapeDtyp...  14.5 us

profile of v2, /device:TPU:1, one launch (start us, length us, event | category | flops | bytes accessed | tf_op | source)
XLA Modules:
  0.0 162.8 jit_solution(5209387726001405278)
XLA Ops:
  0.6 14.5 %gram_one.1.x_ref = f32[1280,128]{1,0:T(8,128)} custom-call(f32[4096,512]{1,0:T(8,128)} %a_ref.3), custom_call_target="tpu_custom_call" | custom-call | tf_op jit(solution)/shard_map/gram_one/pallas_call | solution.py:141
  15.2 31.1 %sum_rows.2.g_ref = f32[1280,128]{1,0:T(8,128)} custom-call(f32[1280,128]{1,0:T(8,128)} %gram_one.1.x_ref), custom_call_target="tpu_custom_call" | custom-call | tf_op jit(solution)/shard_map/sum_rows/pallas_call | solution.py:94
  46.2 21.6 %chol_one.1 = (f32[512,512]{1,0:T(8,128)}, f32[512,256]{1,0:T(8,128)}) custom-call(f32[1280,128]{1,0:T(8,128)} %sum_rows.2.g_ref), custom_call_target="tpu_custom_call" | custom-call | tf_op jit(solution)/shard_map/chol_one/pallas_call | solution.py:262
  67.8 37.9 %second_pass.1.x_ref = f32[1792,128]{1,0:T(8,128)} custom-call(f32[4096,512]{1,0:T(8,128)} %a_ref.3, f32[4096,128]{1,0:T(8,128)} %b_ref.1, f32[512,512]{1,0:T(8,128)} %get-tuple-element.4.r_ref.r_one, f32[512,256]{1,0:T(8,128)} %get-tuple-element.5.x_ref.x_one), custom_call_target="tpu_custom_call" | custom-call | tf_op jit(solution)/shard_map/second_pass/pallas_call | solution.py:176
  105.7 31.1 %sum_rows.3.g_ref = f32[1792,128]{1,0:T(8,128)} custom-call(f32[1792,128]{1,0:T(8,128)} %second_pass.1.x_ref), custom_call_target="tpu_custom_call" | custom-call | tf_op jit(solution)/shard_map/sum_rows/pallas_call | solution.py:94
  136.8 26.0 %finish.1 = (f32[512,128]{1,0:T(8,128)}, f32[512,512]{1,0:T(8,128)}) custom-call(f32[1792,128]{1,0:T(8,128)} %sum_rows.3.g_ref, f32[512,512]{1,0:T(8,128)} %get-tuple-element.4.r_ref.r_one, f32[512,256]{1,0:T(8,128)} %get-tuple-element.5.x_ref.x_one), custom_call_target="tpu_custom_call" | custom-call | tf_op jit(solution)/shard_map/finish/pallas_call | solution.py:292

commit v3 on v2

v3 whole, which is shorter than its diff:
```python
import jax
import jax.numpy as jnp
from jax import lax
from jax.experimental import pallas as pl
from jax.experimental.pallas import tpu as pltpu
from jax.sharding import PartitionSpec as P

HIGHEST = lax.Precision.HIGHEST
CHIPS = 64
CH = 16
TRI = [(j, i) for j in range(4) for i in range(j, 4)]
TILE = 512
GIVE = 60 * 1024 * 1024


def mm(a, b):
    return lax.dot_general(a, b, (((1,), (0,)), ((), ())), precision=HIGHEST, preferred_element_type=jnp.float32)


def mm_t(a, b):
    return lax.dot_general(a, b, (((0,), (0,)), ((), ())), precision=HIGHEST, preferred_element_type=jnp.float32)


def pack_into(o_ref, g_ref):
    for t, (j, i) in enumerate(TRI):
        o_ref[t * 128:t * 128 + 128, :] = g_ref[j * 128:j * 128 + 128, i * 128:i * 128 + 128]


def owner_index(chip, n_own):
    idx = (chip * n_own + CHIPS - 1) // CHIPS
    return idx, jnp.logical_and((idx * CHIPS) // n_own == chip, idx < n_own)


def place():
    dev = lax.axis_index("rows")
    return dev // 2, dev % 2


def peer(chip, core, step):
    t = (chip + step) % CHIPS
    return t, {"rows": t * 2 + core}


def greet(barrier):
    chip, core = place()
    pl.semaphore_signal(barrier, inc=1, device_id={"rows": chip * 2 + 1 - core})

    @pl.loop(1, CHIPS)
    def _(step):
        pl.semaphore_signal(barrier, inc=1, device_id=peer(chip, core, step)[1])


def sum_all(x_ref, o_ref, pair_buf, part, rs_buf, red, sems):
    chip, core = place()
    half = x_ref.shape[0] // 2
    n_own = half // CH
    mine = pl.multiple_of(core * half, CH)
    other = pl.multiple_of((1 - core) * half, CH)
    partner = {"rows": chip * 2 + 1 - core}

    pair = pltpu.make_async_remote_copy(x_ref.at[pl.ds(other, half)], pair_buf, sems.at[0], sems.at[1], device_id=partner)
    pair.start()
    pair.wait()
    part[...] = x_ref[pl.ds(mine, half), :] + pair_buf[...]

    my_idx, owner = owner_index(chip, n_own)
    my_row = pl.multiple_of(my_idx * CH, CH)

    @pl.loop(1, CHIPS)
    def _(step):
        t, dst = peer(chip, core, step)
        idx, owns = owner_index(t, n_own)

        @pl.when(owns)
        def _():
            pltpu.make_async_remote_copy(part.at[pl.ds(pl.multiple_of(idx * CH, CH), CH)],
                                         rs_buf.at[pl.ds(pl.multiple_of((step - 1) * CH, CH), CH)],
                                         sems.at[2], sems.at[3], device_id=dst).start()

    def wait_rows(n, sem):
        pltpu.make_async_copy(part.at[pl.ds(0, n * CH)], part.at[pl.ds(0, n * CH)], sem).wait()

    @pl.when(owner)
    def _():
        pltpu.make_async_copy(rs_buf, rs_buf, sems.at[3]).wait()
        tot = part[pl.ds(my_row, CH), :]
        for s in range(CHIPS - 1):
            tot = tot + rs_buf[pl.ds(s * CH, CH), :]
        red[...] = tot
        o_ref[pl.ds(mine + my_row, CH), :] = tot

        @pl.loop(1, CHIPS)
        def _(step):
            pltpu.make_async_remote_copy(red, o_ref.at[pl.ds(pl.multiple_of(mine + my_row, CH), CH)],
                                         sems.at[4], sems.at[5], device_id=peer(chip, core, step)[1]).start()
        wait_rows(n_own - 1, sems.at[2])
        wait_rows(n_own - 1, sems.at[5])

    @pl.when(jnp.logical_not(owner))
    def _():
        wait_rows(n_own, sems.at[2])
        wait_rows(n_own, sems.at[5])

    swap = pltpu.make_async_remote_copy(o_ref.at[pl.ds(mine, half)], o_ref.at[pl.ds(mine, half)], sems.at[6], sems.at[7], device_id=partner)
    swap.start()
    swap.wait()

    @pl.when(owner)
    def _():
        pltpu.make_async_copy(rs_buf, rs_buf, sems.at[4]).wait()


def factor_block(d_mat):
    sub = lax.broadcasted_iota(jnp.int32, (8, 128), 0)
    lane = lax.broadcasted_iota(jnp.int32, (8, 128), 1)
    d_row = lax.broadcasted_iota(jnp.int32, (128, 128), 0)
    d_col = lax.broadcasted_iota(jnp.int32, (128, 128), 1)
    d_mat = jnp.where(d_col >= d_row, d_mat, d_mat.T)
    rows = [d_mat[8 * i:8 * i + 8, :] for i in range(16)]
    inv = [jnp.where(lane == sub + 8 * i, 1.0, 0.0).astype(jnp.float32) for i in range(16)]
    r_out, v_out = [], []
    for k in range(16):
        cols = {i: [jnp.broadcast_to(rows[i][:, 8 * k + r:8 * k + r + 1], (8, 128)) for r in range(8)] for i in range(k, 16)}
        scale = jnp.zeros((8, 128), jnp.float32)
        top = cols[k]
        for r in range(8):
            inv_root = lax.rsqrt(jnp.broadcast_to(top[r][r:r + 1, :], (8, 128)))
            scale = jnp.where(sub == r, inv_root, scale)
            below = jnp.where(sub > r, top[r] * inv_root, 0.0)
            row_s = jnp.broadcast_to(rows[k][r:r + 1, :], (8, 128)) * inv_root
            row_v = jnp.broadcast_to(inv[k][r:r + 1, :], (8, 128)) * inv_root
            coef = [jnp.broadcast_to(top[c][r:r + 1, :], (8, 128)) * inv_root for c in range(r + 1, 8)]
            for c in range(r + 1, 8):
                top[c] = top[c] - below * coef[c - r - 1]
            rows[k] = rows[k] - below * row_s
            inv[k] = inv[k] - below * row_v
            for i in range(k + 1, 16):
                mult = cols[i][r] * inv_root
                for c in range(r + 1, 8):
                    cols[i][c] = cols[i][c] - mult * coef[c - r - 1]
                rows[i] = rows[i] - mult * row_s
                inv[i] = inv[i] - mult * row_v
        r_out.append(jnp.where(lane >= sub + 8 * k, rows[k] * scale, 0.0))
        v_out.append(inv[k] * scale)
    return r_out, v_out


def factor(g_ref, r_out, x_out, s_mat, v_mat, r_mat):
    width = s_mat.shape[1]
    for t, (j, i) in enumerate(TRI):
        s_mat[j * 128:j * 128 + 128, i * 128:i * 128 + 128] = g_ref[t * 128:t * 128 + 128, :]
    if width > 512:
        s_mat[:, 512:] = g_ref[1280:, :]

    @pl.loop(0, 4)
    def _(j):
        top = pl.multiple_of(j * 128, 128)
        r_blk, v_blk = factor_block(s_mat[pl.ds(top, 128), pl.ds(top, 128)])
        for i in range(16):
            r_mat[pl.ds(top + 8 * i, 8), pl.ds(top, 128)] = r_blk[i]
            v_mat[pl.ds(top + 8 * i, 8), :] = v_blk[i]
        for jj in range(4):
            lo, hi = 128 * jj, 128 * jj + 128
            if hi < width:
                @pl.when(j == jj)
                def _():
                    row = mm(v_mat[lo:hi, :], s_mat[lo:hi, hi:])
                    r_mat[lo:hi, hi:] = row
                    if hi < 512:
                        s_mat[hi:, hi:] = s_mat[hi:, hi:] - mm_t(row[:, :512 - hi], row)
    for jj in range(1, 4):
        r_mat[128 * jj:128 * jj + 128, :128 * jj] = jnp.zeros((128, 128 * jj), jnp.float32)
    for p in range(2):
        lo, mid, hi = 256 * p, 256 * p + 128, 256 * p + 256
        x_lo, x_hi = v_mat[lo:mid, :].T, v_mat[mid:hi, :].T
        x_out[lo:mid, :128] = x_lo
        x_out[mid:hi, 128:] = x_hi
        x_out[mid:hi, :128] = jnp.zeros((128, 128), jnp.float32)
        x_out[lo:mid, 128:] = -mm(x_lo, mm(r_mat[lo:mid, mid:hi], x_hi))


def back_solve(r_ref, x_ref, y_lo, y_hi):
    z_hi = mm(x_ref[256:, :], y_hi)
    z_lo = mm(x_ref[:256, :], y_lo - mm(r_ref[:256, 256:512], z_hi))
    return z_lo, z_hi


def solve_kernel(a_hbm, b_hbm, sol, r_fac, a_buf, b_buf, acc, proj, x_g, o_g, x_h, o_h, pair_g, part_g, rs_g, red_g,
                 pair_h, part_h, rs_h, red_h, s_one, v_one, r_one, x_one, s_two, v_two, r_two, x_two, load_sem, sems_g, sems_h):
    rows = a_hbm.shape[0]
    steps = rows // TILE

    def tile(i):
        return pl.ds(pl.multiple_of(i * TILE, TILE), TILE)

    def load_a(i):
        return pltpu.make_async_copy(a_hbm.at[tile(i)], a_buf.at[tile(i)], load_sem.at[i])

    load_b = pltpu.make_async_copy(b_hbm, b_buf, load_sem.at[steps])
    for i in range(steps):
        load_a(i).start()
    load_b.start()
    barrier = pltpu.get_barrier_semaphore()
    greet(barrier)

    acc[...] = jnp.zeros_like(acc)

    @pl.loop(0, steps)
    def _(i):
        load_a(i).wait()
        a_lo, a_hi = a_buf[tile(i), :256], a_buf[tile(i), 256:]
        acc[:256, :] += mm_t(a_lo, a_buf[tile(i), :])
        acc[256:, 256:] += mm_t(a_hi, a_hi)
    pack_into(x_g, acc)
    pl.semaphore_wait(barrier, CHIPS)
    sum_all(x_g, o_g, pair_g, part_g, rs_g, red_g, sems_g)
    factor(o_g, r_one, x_one, s_one, v_one, r_one)

    acc[...] = jnp.zeros_like(acc)
    proj[...] = jnp.zeros_like(proj)
    load_b.wait()

    @pl.loop(0, steps)
    def _(i):
        q_lo = mm(a_buf[tile(i), :256], x_one[:256, :])
        q_hi = mm(a_buf[tile(i), 256:] - mm(q_lo, r_one[:256, 256:]), x_one[256:, :])
        b_blk = b_buf[tile(i), :]
        acc[:256, :256] += mm_t(q_lo, q_lo)
        acc[:256, 256:] += mm_t(q_lo, q_hi)
        acc[256:, 256:] += mm_t(q_hi, q_hi)
        proj[:256, :] += mm_t(q_lo, b_blk)
        proj[256:, :] += mm_t(q_hi, b_blk)
    pack_into(x_h, acc)
    x_h[1280:, :] = proj[...]
    sum_all(x_h, o_h, pair_h, part_h, rs_h, red_h, sems_h)
    factor(o_h, r_two, x_two, s_two, v_two, r_two)

    z_lo, z_hi = back_solve(r_two, x_two, r_two[:256, 512:], r_two[256:, 512:])
    s_lo, s_hi = back_solve(r_one, x_one, z_lo, z_hi)
    sol[:256, :] = s_lo
    sol[256:, :] = s_hi
    r_fac[:256, :256] = mm(r_two[:256, :256], r_one[:256, :256])
    r_fac[:256, 256:] = mm(r_two[:256, :512], r_one[:, 256:])
    r_fac[256:, 256:] = mm(r_two[256:, 256:512], r_one[256:, 256:])
    r_fac[256:, :256] = jnp.zeros((256, 256), jnp.float32)


def solution(mesh):
    def group_solve(a_blk, b_blk):
        rows = a_blk.shape[0]

        def buf(r, c=128):
            return pltpu.VMEM((r, c), jnp.float32)

        def sums(r):
            return [buf(r // 2), buf(r // 2), buf((CHIPS - 1) * CH), buf(CH)]
        return pl.pallas_call(
            solve_kernel,
            out_shape=(jax.ShapeDtypeStruct((512, 128), jnp.float32), jax.ShapeDtypeStruct((512, 512), jnp.float32)),
            in_specs=[pl.BlockSpec(memory_space=pl.ANY)] * 2,
            out_specs=(pl.BlockSpec(memory_space=pltpu.VMEM),) * 2,
            scratch_shapes=[buf(rows, 512), buf(rows), buf(512, 512), buf(512), buf(1280), buf(1280), buf(1792), buf(1792),
                            *sums(1280), *sums(1792),
                            buf(512, 512), buf(512), buf(512, 512), buf(512, 256),
                            buf(512, 640), buf(512), buf(512, 640), buf(512, 256),
                            pltpu.SemaphoreType.DMA((rows // TILE + 1,)), pltpu.SemaphoreType.DMA((8,)), pltpu.SemaphoreType.DMA((8,))],
            compiler_params=pltpu.CompilerParams(collective_id=0, has_side_effects=True, vmem_limit_bytes=GIVE),
            name="solve",
        )(a_blk, b_blk)

    row_spec = P(("batch", "rows"), None)
    out_spec = P("batch", None)
    return jax.shard_map(group_solve, mesh=mesh, in_specs=(row_spec, row_spec), out_specs=(out_spec, out_spec), check_vma=False)
```

time: 163 us -> 146 us (0.90)
  Pallas kernels: 162 us -> 141 us
  local copies, waits for them, and re-layouts: 0 us -> 3.93 us
    pallas_call x6 -> x1, Pallas kernels: 162 us -> 141 us  [group_solve(): pl.pallas_call(solve_kernel, out_shape=(jax.ShapeDtypeStruct((512, 128),...]
    unnamed x0 -> x2, local copies, waits for them, and re-layouts: none -> 3.93 us
where the time goes in v3:
time: 146 us
  Pallas kernels  141 us (97%)
  local copies, waits for them, and re-layouts  3.93 us (3%)
    pallas_call x1, Pallas kernels, group_solve(): pl.pallas_call(solve_kernel, out_shape=(jax.ShapeDtypeStruct((512, 128),...  141 us
    unnamed x2, local copies, waits for them, and re-layouts  3.93 us

profile of v3, /device:TPU:1, one launch (start us, length us, event | category | flops | bytes accessed | tf_op | source)
XLA Modules:
  0.0 145.5 jit_solution(5486744209742301793)
XLA Ops:
  0.6 141.0 %solve.1 = (f32[512,128]{1,0:T(8,128)}, f32[512,512]{1,0:T(8,128)}) custom-call(f32[4096,512]{1,0:T(8,128)} %a_hbm.1, f32[4096,128]{1,0:T(8,128)} %b_hbm.1), custom_call_target="tpu_custom_call" | custom-call | tf_op jit(solution)/shard_map/solve/pallas_call | solution.py:257
  141.6 1.7 %copy.6 = f32[512,128]{1,0:T(8,128)} copy(f32[512,128]{1,0:T(8,128)} %get-tuple-element.4) | data formatting | bytes 524288
  143.3 2.3 %copy.7 = f32[512,512]{1,0:T(8,128)} copy(f32[512,512]{1,0:T(8,128)} %get-tuple-element.5) | data formatting | bytes 2097152

commit v4 on v3

v4 whole, which is shorter than its diff:
```python
import jax
import jax.numpy as jnp
from jax import lax
from jax.experimental import pallas as pl
from jax.experimental.pallas import tpu as pltpu
from jax.sharding import PartitionSpec as P

HIGHEST = lax.Precision.HIGHEST
CHIPS = 64
CH = 8
SPREAD, UNSPREAD = 27, 19
LOAD = 512
TILE = 1024
GIVE = 60 * 1024 * 1024
LOLO = [(0, 0), (0, 1), (1, 1)]
LOHI = [(0, 2), (0, 3), (1, 2), (1, 3)]
HIHI = [(2, 2), (2, 3), (3, 3)]


def mm(a, b):
    return lax.dot_general(a, b, (((1,), (0,)), ((), ())), precision=HIGHEST, preferred_element_type=jnp.float32)


def mm_t(a, b):
    return lax.dot_general(a, b, (((0,), (0,)), ((), ())), precision=HIGHEST, preferred_element_type=jnp.float32)


def block(ref, j, i):
    return ref.at[j * 128:j * 128 + 128, i * 128:i * 128 + 128]


def place():
    dev = lax.axis_index("rows")
    return dev // 2, dev % 2


def greet(barrier):
    chip, core = place()
    pl.semaphore_signal(barrier, inc=1, device_id={"rows": chip * 2 + 1 - core})

    @pl.loop(1, CHIPS)
    def _(step):
        pl.semaphore_signal(barrier, inc=1, device_id={"rows": ((chip + step) % CHIPS) * 2 + core})


class Piece:
    def __init__(self, refs, offset):
        self.x, self.o, self.pair_buf, self.part, self.rs_buf, self.red, self.sems = refs
        self.offset = offset
        self.half = self.x.shape[0] // 2
        self.n_own = self.half // CH
        self.chip, self.core = place()
        self.mine = pl.multiple_of(self.core * self.half, CH)
        self.other = pl.multiple_of((1 - self.core) * self.half, CH)
        self.partner = {"rows": self.chip * 2 + 1 - self.core}
        self.idx = (self.chip * UNSPREAD + CHIPS - offset % CHIPS) % CHIPS
        self.owner = self.idx < self.n_own
        self.row = pl.multiple_of(self.idx * CH, CH)

    def swap_in(self):
        return pltpu.make_async_remote_copy(self.x.at[pl.ds(self.other, self.half)], self.pair_buf,
                                            self.sems.at[0], self.sems.at[1], device_id=self.partner)

    def swap_out(self):
        here = self.o.at[pl.ds(self.mine, self.half)]
        return pltpu.make_async_remote_copy(here, here, self.sems.at[6], self.sems.at[7], device_id=self.partner)

    def rows_of(self, n):
        return self.part.at[pl.ds(0, n * CH)]

    def start(self):
        self.swap_in().start()

    def scatter(self):
        self.swap_in().wait()
        self.part[...] = self.x[pl.ds(self.mine, self.half), :] + self.pair_buf[...]

        @pl.loop(0, self.n_own)
        def _(step):
            j = (step + self.chip) % self.n_own
            t = ((j + self.offset) * SPREAD) % CHIPS
            slot = (self.chip + CHIPS - t) % CHIPS - 1

            @pl.when(t != self.chip)
            def _():
                pltpu.make_async_remote_copy(self.part.at[pl.ds(pl.multiple_of(j * CH, CH), CH)],
                                             self.rs_buf.at[pl.ds(pl.multiple_of(slot * CH, CH), CH)],
                                             self.sems.at[2], self.sems.at[3], device_id={"rows": t * 2 + self.core}).start()

    def gather(self):
        @pl.when(self.owner)
        def _():
            pltpu.make_async_copy(self.rs_buf, self.rs_buf, self.sems.at[3]).wait()
            lanes = [self.part[pl.ds(self.row, CH), :]] + [self.rs_buf[s * CH:s * CH + CH, :] for s in range(CHIPS - 1)]
            while len(lanes) > 1:
                lanes = [u + v for u, v in zip(lanes[::2], lanes[1::2])]
            self.red[...] = lanes[0]
            self.o[pl.ds(self.mine + self.row, CH), :] = lanes[0]
            there = self.o.at[pl.ds(pl.multiple_of(self.mine + self.row, CH), CH)]

            @pl.loop(1, CHIPS)
            def _(step):
                pltpu.make_async_remote_copy(self.red, there, self.sems.at[4], self.sems.at[5],
                                             device_id={"rows": ((self.chip + step) % CHIPS) * 2 + self.core}).start()

    def spread(self):
        for own, n in ((True, self.n_own - 1), (False, self.n_own)):
            @pl.when(self.owner == own)
            def _():
                pltpu.make_async_copy(self.rows_of(n), self.rows_of(n), self.sems.at[5]).wait()
        self.swap_out().start()

    def finish(self):
        self.swap_out().wait()
        for own, n in ((True, self.n_own - 1), (False, self.n_own)):
            @pl.when(self.owner == own)
            def _():
                pltpu.make_async_copy(self.rows_of(n), self.rows_of(n), self.sems.at[2]).wait()

        @pl.when(self.owner)
        def _():
            pltpu.make_async_copy(self.rs_buf, self.rs_buf, self.sems.at[4]).wait()


def pack(ref, blocks):
    for t, blk in enumerate(blocks):
        ref[t * 128:t * 128 + 128, :] = blk[...]


def piece_block(ref, t):
    return ref[t * 128:t * 128 + 128, :]


def factor_block(d_mat):
    sub = lax.broadcasted_iota(jnp.int32, (8, 128), 0)
    lane = lax.broadcasted_iota(jnp.int32, (8, 128), 1)
    d_row = lax.broadcasted_iota(jnp.int32, (128, 128), 0)
    d_col = lax.broadcasted_iota(jnp.int32, (128, 128), 1)
    d_mat = jnp.where(d_col >= d_row, d_mat, d_mat.T)
    rows = [d_mat[8 * i:8 * i + 8, :] for i in range(16)]
    inv = [jnp.where(lane == sub + 8 * i, 1.0, 0.0).astype(jnp.float32) for i in range(16)]
    r_out, v_out = [], []
    for k in range(16):
        cols = {i: [jnp.broadcast_to(rows[i][:, 8 * k + r:8 * k + r + 1], (8, 128)) for r in range(8)] for i in range(k, 16)}
        scale = jnp.zeros((8, 128), jnp.float32)
        top = cols[k]
        for r in range(8):
            inv_root = lax.rsqrt(jnp.broadcast_to(top[r][r:r + 1, :], (8, 128)))
            scale = jnp.where(sub == r, inv_root, scale)
            below = jnp.where(sub > r, top[r] * inv_root, 0.0)
            row_s = jnp.broadcast_to(rows[k][r:r + 1, :], (8, 128)) * inv_root
            row_v = jnp.broadcast_to(inv[k][r:r + 1, :], (8, 128)) * inv_root
            coef = [jnp.broadcast_to(top[c][r:r + 1, :], (8, 128)) * inv_root for c in range(r + 1, 8)]
            for c in range(r + 1, 8):
                top[c] = top[c] - below * coef[c - r - 1]
            rows[k] = rows[k] - below * row_s
            inv[k] = inv[k] - below * row_v
            for i in range(k + 1, 16):
                mult = cols[i][r] * inv_root
                for c in range(r + 1, 8):
                    cols[i][c] = cols[i][c] - mult * coef[c - r - 1]
                rows[i] = rows[i] - mult * row_s
                inv[i] = inv[i] - mult * row_v
        r_out.append(jnp.where(lane >= sub + 8 * k, rows[k] * scale, 0.0))
        v_out.append(inv[k] * scale)
    return r_out, v_out


def factor(pieces, r_mat, x_out, s_mat, v_mat):
    width = s_mat.shape[1]
    p_lo, p_mid, p_hi = pieces
    s_mat[256:, 256:] = jnp.zeros((256, width - 256), jnp.float32)
    p_lo.finish()
    for t, (j, i) in enumerate(LOLO):
        block(s_mat, j, i)[...] = piece_block(p_lo.o, t)
    if width > 512:
        for t in range(2):
            block(s_mat, t, 4)[...] = piece_block(p_lo.o, 3 + t).T

    @pl.loop(0, 4)
    def _(j):
        top = pl.multiple_of(j * 128, 128)

        @pl.when(j == 2)
        def _():
            p_hi.finish()
            for t, (jj, ii) in enumerate(HIHI):
                block(s_mat, jj, ii)[...] += piece_block(p_hi.o, t)
            if width > 512:
                for t in range(2):
                    block(s_mat, 2 + t, 4)[...] += piece_block(p_hi.o, 3 + t).T
        r_blk, v_blk = factor_block(s_mat[pl.ds(top, 128), pl.ds(top, 128)])
        for i in range(16):
            r_mat[pl.ds(top + 8 * i, 8), pl.ds(top, 128)] = r_blk[i]
            v_mat[pl.ds(top + 8 * i, 8), :] = v_blk[i]

        @pl.when(j == 0)
        def _():
            p_mid.spread()
            p_hi.gather()
            p_mid.finish()
            for t, (jj, ii) in enumerate(LOHI):
                block(s_mat, jj, ii)[...] = piece_block(p_mid.o, t)

        @pl.when(j == 1)
        def _():
            p_hi.spread()
        for jj in range(4):
            lo, hi = 128 * jj, 128 * jj + 128
            if hi < width:
                @pl.when(j == jj)
                def _():
                    row = mm(v_mat[lo:hi, :], s_mat[lo:hi, hi:])
                    r_mat[lo:hi, hi:] = row
                    if hi < 512:
                        s_mat[hi:, hi:] = s_mat[hi:, hi:] - mm_t(row[:, :512 - hi], row)
    for jj in range(1, 4):
        r_mat[128 * jj:128 * jj + 128, :128 * jj] = jnp.zeros((128, 128 * jj), jnp.float32)
    for p in range(2):
        lo, mid, hi = 256 * p, 256 * p + 128, 256 * p + 256
        x_lo, x_hi = v_mat[lo:mid, :].T, v_mat[mid:hi, :].T
        x_out[lo:mid, :128] = x_lo
        x_out[mid:hi, 128:] = x_hi
        x_out[mid:hi, :128] = jnp.zeros((128, 128), jnp.float32)
        x_out[lo:mid, 128:] = -mm(x_lo, mm(r_mat[lo:mid, mid:hi], x_hi))


def back_solve(r_ref, x_ref, y_lo, y_hi):
    z_hi = mm(x_ref[256:, :], y_hi)
    z_lo = mm(x_ref[:256, :], y_lo - mm(r_ref[:256, 256:512], z_hi))
    return z_lo, z_hi


def solve_kernel(a_hbm, b_hbm, sol, r_fac, a_buf, b_buf, acc, proj, *refs):
    piece_refs, (s_one, v_one, r_one, x_one, s_two, v_two, r_two, x_two, load_sem) = refs[:42], refs[42:]
    one = [Piece(piece_refs[7 * p:7 * p + 7], off) for p, off in enumerate((0, 24, 56))]
    two = [Piece(piece_refs[7 * p:7 * p + 7], off) for p, off in zip((3, 4, 5), (0, 40, 72))]
    rows = a_hbm.shape[0]
    steps = rows // TILE

    def tile(i, size=TILE):
        return pl.ds(pl.multiple_of(i * size, size), size)

    def load_a(i):
        return pltpu.make_async_copy(a_hbm.at[tile(i, LOAD)], a_buf.at[tile(i, LOAD)], load_sem.at[i])

    load_b = pltpu.make_async_copy(b_hbm, b_buf, load_sem.at[rows // LOAD])
    for i in range(rows // LOAD):
        load_a(i).start()
    load_b.start()
    barrier = pltpu.get_barrier_semaphore()
    greet(barrier)
    acc[...] = jnp.zeros_like(acc)
    proj[...] = jnp.zeros_like(proj)

    @pl.loop(0, steps)
    def _(i):
        for part in range(TILE // LOAD):
            load_a(i * (TILE // LOAD) + part).wait()
        a_lo = a_buf[tile(i), :256]
        acc[:256, :256] += mm_t(a_lo, a_lo)
    pack(one[0].x, [block(acc, *ij) for ij in LOLO])
    pl.semaphore_wait(barrier, CHIPS)
    one[0].start()

    @pl.loop(0, steps)
    def _(i):
        acc[:256, 256:] += mm_t(a_buf[tile(i), :256], a_buf[tile(i), 256:])

        @pl.when(i == 1)
        def _():
            one[0].scatter()
    pack(one[1].x, [block(acc, *ij) for ij in LOHI])
    one[1].start()

    @pl.loop(0, steps)
    def _(i):
        a_hi = a_buf[tile(i), 256:]
        acc[256:, 256:] += mm_t(a_hi, a_hi)

        @pl.when(i == 1)
        def _():
            one[1].scatter()

        @pl.when(i == 2)
        def _():
            one[0].gather()
    pack(one[2].x, [block(acc, *ij) for ij in HIHI])
    one[2].start()
    one[1].gather()
    one[2].scatter()
    one[0].spread()
    factor(one, r_one, x_one, s_one, v_one)

    acc[...] = jnp.zeros_like(acc)
    load_b.wait()

    @pl.loop(0, steps)
    def _(i):
        q_lo = mm(a_buf[tile(i), :256], x_one[:256, :])
        a_buf[tile(i), :256] = q_lo
        acc[:256, :256] += mm_t(q_lo, q_lo)
        proj[:, :256] += mm_t(b_buf[tile(i), :], q_lo)
    pack(two[0].x, [block(acc, *ij) for ij in LOLO] + [block(proj, 0, i) for i in range(2)])
    two[0].start()

    @pl.loop(0, steps)
    def _(i):
        q_lo = a_buf[tile(i), :256]
        q_hi = mm(a_buf[tile(i), 256:] - mm(q_lo, r_one[:256, 256:]), x_one[256:, :])
        a_buf[tile(i), 256:] = q_hi
        acc[:256, 256:] += mm_t(q_lo, q_hi)

        @pl.when(i == 0)
        def _():
            two[0].scatter()

        @pl.when(i == 2)
        def _():
            two[0].gather()
    pack(two[1].x, [block(acc, *ij) for ij in LOHI])
    two[1].start()

    @pl.loop(0, steps)
    def _(i):
        q_hi = a_buf[tile(i), 256:]
        acc[256:, 256:] += mm_t(q_hi, q_hi)
        proj[:, 256:] += mm_t(b_buf[tile(i), :], q_hi)

        @pl.when(i == 0)
        def _():
            two[1].scatter()

        @pl.when(i == 1)
        def _():
            two[0].spread()
    pack(two[2].x, [block(acc, *ij) for ij in HIHI] + [block(proj, 0, i) for i in range(2, 4)])
    two[2].start()
    two[1].gather()
    two[2].scatter()
    factor(two, r_two, x_two, s_two, v_two)

    z_lo, z_hi = back_solve(r_two, x_two, r_two[:256, 512:], r_two[256:, 512:])
    s_lo, s_hi = back_solve(r_one, x_one, z_lo, z_hi)
    sol[:256, :] = s_lo
    sol[256:, :] = s_hi
    r_fac[:256, :256] = mm(r_two[:256, :256], r_one[:256, :256])
    r_fac[:256, 256:] = mm(r_two[:256, :512], r_one[:, 256:])
    r_fac[256:, 256:] = mm(r_two[256:, 256:512], r_one[256:, 256:])
    r_fac[256:, :256] = jnp.zeros((256, 256), jnp.float32)


def solution(mesh):
    def group_solve(a_blk, b_blk):
        rows = a_blk.shape[0]

        def buf(r, c=128):
            return pltpu.VMEM((r, c), jnp.float32)

        def piece(r):
            return [buf(r), buf(r), buf(r // 2), buf(r // 2), buf((CHIPS - 1) * CH), buf(CH), pltpu.SemaphoreType.DMA((8,))]
        return pl.pallas_call(
            solve_kernel,
            out_shape=(jax.ShapeDtypeStruct((512, 128), jnp.float32), jax.ShapeDtypeStruct((512, 512), jnp.float32)),
            in_specs=[pl.BlockSpec(memory_space=pl.ANY)] * 2,
            out_specs=(pl.BlockSpec(memory_space=pltpu.VMEM),) * 2,
            scratch_shapes=[buf(rows, 512), buf(rows), buf(512, 512), buf(128, 512),
                            *piece(384), *piece(512), *piece(384), *piece(640), *piece(512), *piece(640),
                            buf(512, 512), buf(512), buf(512, 512), buf(512, 256),
                            buf(512, 640), buf(512), buf(512, 640), buf(512, 256),
                            pltpu.SemaphoreType.DMA((rows // LOAD + 1,))],
            compiler_params=pltpu.CompilerParams(collective_id=0, has_side_effects=True, vmem_limit_bytes=GIVE),
            name="solve",
        )(a_blk, b_blk)

    row_spec = P(("batch", "rows"), None)
    out_spec = P("batch", None)
    return jax.shard_map(group_solve, mesh=mesh, in_specs=(row_spec, row_spec), out_specs=(out_spec, out_spec), check_vma=False)
```

time: 146 us -> 127 us (0.87)
  Pallas kernels: 141 us -> 122 us
    pallas_call x1, Pallas kernels: 141 us -> 122 us  [group_solve(): pl.pallas_call(solve_kernel, out_shape=(jax.ShapeDtypeStruct((512, 128),...]
where the time goes in v4:
time: 127 us; the launch traced here: 126 us
  Pallas kernels  122 us (96%)
  local copies, waits for them, and re-layouts  3.93 us (3%)
    pallas_call x1, Pallas kernels, group_solve(): pl.pallas_call(solve_kernel, out_shape=(jax.ShapeDtypeStruct((512, 128),...  122 us
    unnamed x2, local copies, waits for them, and re-layouts  3.93 us

profile of v4, /device:TPU:1, one launch (start us, length us, event | category | flops | bytes accessed | tf_op | source)
XLA Modules:
  0.0 126.3 jit_solution(17625505248441205825)
XLA Ops:
  0.6 121.8 %solve.1 = (f32[512,128]{1,0:T(8,128)}, f32[512,512]{1,0:T(8,128)}) custom-call(f32[4096,512]{1,0:T(8,128)} %a_hbm.1, f32[4096,128]{1,0:T(8,128)} %b_hbm.1), custom_call_target="tpu_custom_call" | custom-call | tf_op jit(solution)/shard_map/solve/pallas_call | solution.py:362
  122.4 1.7 %copy.6 = f32[512,128]{1,0:T(8,128)} copy(f32[512,128]{1,0:T(8,128)} %get-tuple-element.4) | data formatting | bytes 524288
  124.1 2.3 %copy.7 = f32[512,512]{1,0:T(8,128)} copy(f32[512,512]{1,0:T(8,128)} %get-tuple-element.5) | data formatting | bytes 2097152

commit v5 on v4

--- a/solution.py
+++ b/solution.py
@@ -11,6 +11,7 @@
 SPREAD, UNSPREAD = 27, 19
 LOAD = 512
 TILE = 1024
+WIDE = 2048
 GIVE = 60 * 1024 * 1024
 LOLO = [(0, 0), (0, 1), (1, 1)]
 LOHI = [(0, 2), (0, 3), (1, 2), (1, 3)]
@@ -219,19 +220,15 @@
     for p in range(2):
         lo, mid, hi = 256 * p, 256 * p + 128, 256 * p + 256
         x_lo, x_hi = v_mat[lo:mid, :].T, v_mat[mid:hi, :].T
-        x_out[lo:mid, :128] = x_lo
-        x_out[mid:hi, 128:] = x_hi
-        x_out[mid:hi, :128] = jnp.zeros((128, 128), jnp.float32)
-        x_out[lo:mid, 128:] = -mm(x_lo, mm(r_mat[lo:mid, mid:hi], x_hi))
-
-
-def back_solve(r_ref, x_ref, y_lo, y_hi):
-    z_hi = mm(x_ref[256:, :], y_hi)
-    z_lo = mm(x_ref[:256, :], y_lo - mm(r_ref[:256, 256:512], z_hi))
-    return z_lo, z_hi
-
-
-def solve_kernel(a_hbm, b_hbm, sol, r_fac, a_buf, b_buf, acc, proj, *refs):
+        x_out[lo:mid, lo:mid] = x_lo
+        x_out[mid:hi, mid:hi] = x_hi
+        x_out[mid:hi, lo:mid] = jnp.zeros((128, 128), jnp.float32)
+        x_out[lo:mid, mid:hi] = -mm(x_lo, mm(r_mat[lo:mid, mid:hi], x_hi))
+    x_out[256:, :256] = jnp.zeros((256, 256), jnp.float32)
+    x_out[:256, 256:] = -mm(mm(x_out[:256, :256], r_mat[:256, 256:512]), x_out[256:, 256:])
+
+
+def solve_kernel(a_hbm, b_hbm, sol, r_fac, a_buf, q_lo, b_buf, acc, proj, *refs):
     piece_refs, (s_one, v_one, r_one, x_one, s_two, v_two, r_two, x_two, load_sem) = refs[:42], refs[42:]
     one = [Piece(piece_refs[7 * p:7 * p + 7], off) for p, off in enumerate((0, 24, 56))]
     two = [Piece(piece_refs[7 * p:7 * p + 7], off) for p, off in zip((3, 4, 5), (0, 40, 72))]
@@ -253,21 +250,24 @@
     acc[...] = jnp.zeros_like(acc)
     proj[...] = jnp.zeros_like(proj)
 
-    @pl.loop(0, steps)
-    def _(i):
-        for part in range(TILE // LOAD):
-            load_a(i * (TILE // LOAD) + part).wait()
-        a_lo = a_buf[tile(i), :256]
+    @pl.loop(0, rows // WIDE)
+    def _(i):
+        for part in range(WIDE // LOAD):
+            load_a(i * (WIDE // LOAD) + part).wait()
+        a_lo = a_buf[tile(i, WIDE), :256]
         acc[:256, :256] += mm_t(a_lo, a_lo)
     pack(one[0].x, [block(acc, *ij) for ij in LOLO])
-    pl.semaphore_wait(barrier, CHIPS)
-    one[0].start()
 
     @pl.loop(0, steps)
     def _(i):
         acc[:256, 256:] += mm_t(a_buf[tile(i), :256], a_buf[tile(i), 256:])
 
         @pl.when(i == 1)
+        def _():
+            pl.semaphore_wait(barrier, CHIPS)
+            one[0].start()
+
+        @pl.when(i == 2)
         def _():
             one[0].scatter()
     pack(one[1].x, [block(acc, *ij) for ij in LOHI])
@@ -278,7 +278,7 @@
         a_hi = a_buf[tile(i), 256:]
         acc[256:, 256:] += mm_t(a_hi, a_hi)
 
-        @pl.when(i == 1)
+        @pl.when(i == 0)
         def _():
             one[1].scatter()
 
@@ -287,35 +287,39 @@
             one[0].gather()
     pack(one[2].x, [block(acc, *ij) for ij in HIHI])
     one[2].start()
+    one[2].scatter()
     one[1].gather()
-    one[2].scatter()
     one[0].spread()
     factor(one, r_one, x_one, s_one, v_one)
 
     acc[...] = jnp.zeros_like(acc)
     load_b.wait()
 
-    @pl.loop(0, steps)
-    def _(i):
-        q_lo = mm(a_buf[tile(i), :256], x_one[:256, :])
-        a_buf[tile(i), :256] = q_lo
-        acc[:256, :256] += mm_t(q_lo, q_lo)
-        proj[:, :256] += mm_t(b_buf[tile(i), :], q_lo)
+    @pl.loop(0, rows // WIDE)
+    def _(i):
+        q_lo[tile(i, WIDE), :] = mm(a_buf[tile(i, WIDE), :256], x_one[:256, :256])
+
+    @pl.loop(0, rows // WIDE)
+    def _(i):
+        q_blk = q_lo[tile(i, WIDE), :]
+        acc[:256, :256] += mm_t(q_blk, q_blk)
+        proj[:, :256] += mm_t(b_buf[tile(i, WIDE), :], q_blk)
     pack(two[0].x, [block(acc, *ij) for ij in LOLO] + [block(proj, 0, i) for i in range(2)])
     two[0].start()
 
-    @pl.loop(0, steps)
-    def _(i):
-        q_lo = a_buf[tile(i), :256]
-        q_hi = mm(a_buf[tile(i), 256:] - mm(q_lo, r_one[:256, 256:]), x_one[256:, :])
-        a_buf[tile(i), 256:] = q_hi
-        acc[:256, 256:] += mm_t(q_lo, q_hi)
+    @pl.loop(0, rows // WIDE)
+    def _(i):
+        a_buf[tile(i, WIDE), 256:] = mm(a_buf[tile(i, WIDE), :], x_one[:, 256:])
 
         @pl.when(i == 0)
         def _():
             two[0].scatter()
 
-        @pl.when(i == 2)
+    @pl.loop(0, rows // WIDE)
+    def _(i):
+        acc[:256, 256:] += mm_t(q_lo[tile(i, WIDE), :], a_buf[tile(i, WIDE), 256:])
+
+        @pl.when(i == 0)
         def _():
             two[0].gather()
     pack(two[1].x, [block(acc, *ij) for ij in LOHI])
@@ -336,14 +340,11 @@
             two[0].spread()
     pack(two[2].x, [block(acc, *ij) for ij in HIHI] + [block(proj, 0, i) for i in range(2, 4)])
     two[2].start()
+    two[2].scatter()
     two[1].gather()
-    two[2].scatter()
     factor(two, r_two, x_two, s_two, v_two)
 
-    z_lo, z_hi = back_solve(r_two, x_two, r_two[:256, 512:], r_two[256:, 512:])
-    s_lo, s_hi = back_solve(r_one, x_one, z_lo, z_hi)
-    sol[:256, :] = s_lo
-    sol[256:, :] = s_hi
+    sol[...] = mm(x_one[...], mm(x_two[...], r_two[:, 512:]))
     r_fac[:256, :256] = mm(r_two[:256, :256], r_one[:256, :256])
     r_fac[:256, 256:] = mm(r_two[:256, :512], r_one[:, 256:])
     r_fac[256:, 256:] = mm(r_two[256:, 256:512], r_one[256:, 256:])
@@ -364,10 +365,10 @@
             out_shape=(jax.ShapeDtypeStruct((512, 128), jnp.float32), jax.ShapeDtypeStruct((512, 512), jnp.float32)),
             in_specs=[pl.BlockSpec(memory_space=pl.ANY)] * 2,
             out_specs=(pl.BlockSpec(memory_space=pltpu.VMEM),) * 2,
-            scratch_shapes=[buf(rows, 512), buf(rows), buf(512, 512), buf(128, 512),
+            scratch_shapes=[buf(rows, 512), buf(rows, 256), buf(rows), buf(512, 512), buf(128, 512),
                             *piece(384), *piece(512), *piece(384), *piece(640), *piece(512), *piece(640),
-                            buf(512, 512), buf(512), buf(512, 512), buf(512, 256),
-                            buf(512, 640), buf(512), buf(512, 640), buf(512, 256),
+                            buf(512, 512), buf(512), buf(512, 512), buf(512, 512),
+                            buf(512, 640), buf(512), buf(512, 640), buf(512, 512),
                             pltpu.SemaphoreType.DMA((rows // LOAD + 1,))],
             compiler_params=pltpu.CompilerParams(collective_id=0, has_side_effects=True, vmem_limit_bytes=GIVE),
             name="solve",

time: 127 us -> 121 us (0.953)
  Pallas kernels: 122 us -> 117 us
    pallas_call x1, Pallas kernels: 122 us -> 117 us  [group_solve(): pl.pallas_call(solve_kernel, out_shape=(jax.ShapeDtypeStruct((512, 128),...]
where the time goes in v5:
time: 121 us
  Pallas kernels  117 us (97%)
  local copies, waits for them, and re-layouts  3.93 us (3%)
    pallas_call x1, Pallas kernels, group_solve(): pl.pallas_call(solve_kernel, out_shape=(jax.ShapeDtypeStruct((512, 128),...  117 us
    unnamed x2, local copies, waits for them, and re-layouts  3.93 us

profile of v5, /device:TPU:1, one launch (start us, length us, event | category | flops | bytes accessed | tf_op | source)
XLA Modules:
  0.0 121.3 jit_solution(17169211065325632301)
XLA Ops:
  0.6 116.7 %solve.1 = (f32[512,128]{1,0:T(8,128)}, f32[512,512]{1,0:T(8,128)}) custom-call(f32[4096,512]{1,0:T(8,128)} %a_hbm.1, f32[4096,128]{1,0:T(8,128)} %b_hbm.1), custom_call_target="tpu_custom_call" | custom-call | tf_op jit(solution)/shard_map/solve/pallas_call | solution.py:363
  117.4 1.7 %copy.6 = f32[512,128]{1,0:T(8,128)} copy(f32[512,128]{1,0:T(8,128)} %get-tuple-element.4) | data formatting | bytes 524288
  119.0 2.3 %copy.7 = f32[512,512]{1,0:T(8,128)} copy(f32[512,512]{1,0:T(8,128)} %get-tuple-element.5) | data formatting | bytes 2097152

commit v6 on v5

--- a/solution.py
+++ b/solution.py
@@ -257,17 +257,14 @@
         a_lo = a_buf[tile(i, WIDE), :256]
         acc[:256, :256] += mm_t(a_lo, a_lo)
     pack(one[0].x, [block(acc, *ij) for ij in LOLO])
+    pl.semaphore_wait(barrier, CHIPS)
+    one[0].start()
 
     @pl.loop(0, steps)
     def _(i):
         acc[:256, 256:] += mm_t(a_buf[tile(i), :256], a_buf[tile(i), 256:])
 
-        @pl.when(i == 1)
-        def _():
-            pl.semaphore_wait(barrier, CHIPS)
-            one[0].start()
-
-        @pl.when(i == 2)
+        @pl.when(i == 0)
         def _():
             one[0].scatter()
     pack(one[1].x, [block(acc, *ij) for ij in LOHI])
@@ -280,16 +277,13 @@
 
         @pl.when(i == 0)
         def _():
+            one[0].gather()
             one[1].scatter()
-
-        @pl.when(i == 2)
-        def _():
-            one[0].gather()
     pack(one[2].x, [block(acc, *ij) for ij in HIHI])
     one[2].start()
+    one[0].spread()
     one[2].scatter()
     one[1].gather()
-    one[0].spread()
     factor(one, r_one, x_one, s_one, v_one)
 
     acc[...] = jnp.zeros_like(acc)
@@ -307,9 +301,9 @@
     pack(two[0].x, [block(acc, *ij) for ij in LOLO] + [block(proj, 0, i) for i in range(2)])
     two[0].start()
 
-    @pl.loop(0, rows // WIDE)
-    def _(i):
-        a_buf[tile(i, WIDE), 256:] = mm(a_buf[tile(i, WIDE), :], x_one[:, 256:])
+    @pl.loop(0, steps)
+    def _(i):
+        a_buf[tile(i), 256:] = mm(a_buf[tile(i), :], x_one[:, 256:])
 
         @pl.when(i == 0)
         def _():
@@ -335,13 +329,13 @@
         def _():
             two[1].scatter()
 
-        @pl.when(i == 1)
+        @pl.when(i == 2)
         def _():
             two[0].spread()
     pack(two[2].x, [block(acc, *ij) for ij in HIHI] + [block(proj, 0, i) for i in range(2, 4)])
     two[2].start()
+    two[1].gather()
     two[2].scatter()
-    two[1].gather()
     factor(two, r_two, x_two, s_two, v_two)
 
     sol[...] = mm(x_one[...], mm(x_two[...], r_two[:, 512:]))
@@ -351,6 +345,17 @@
     r_fac[256:, :256] = jnp.zeros((256, 256), jnp.float32)
 
 
+def hand_on(x_in, r_in, x_out, r_out, x_buf, r_buf, sems):
+    copies = [pltpu.make_async_copy(*p, sems.at[i]) for i, p in enumerate(((x_in, x_buf), (r_in, r_buf), (x_buf, x_out), (r_buf, r_out)))]
+    for c in copies[:2]:
+        c.start()
+    for i in range(2):
+        copies[i].wait()
+        copies[2 + i].start()
+    for c in copies[2:]:
+        c.wait()
+
+
 def solution(mesh):
     def group_solve(a_blk, b_blk):
         rows = a_blk.shape[0]
@@ -360,7 +365,7 @@
 
         def piece(r):
             return [buf(r), buf(r), buf(r // 2), buf(r // 2), buf((CHIPS - 1) * CH), buf(CH), pltpu.SemaphoreType.DMA((8,))]
-        return pl.pallas_call(
+        results = pl.pallas_call(
             solve_kernel,
             out_shape=(jax.ShapeDtypeStruct((512, 128), jnp.float32), jax.ShapeDtypeStruct((512, 512), jnp.float32)),
             in_specs=[pl.BlockSpec(memory_space=pl.ANY)] * 2,
@@ -373,6 +378,14 @@
             compiler_params=pltpu.CompilerParams(collective_id=0, has_side_effects=True, vmem_limit_bytes=GIVE),
             name="solve",
         )(a_blk, b_blk)
+        return pl.pallas_call(
+            hand_on,
+            out_shape=tuple(jax.ShapeDtypeStruct(r.shape, r.dtype) for r in results),
+            in_specs=[pl.BlockSpec(memory_space=pl.ANY)] * 2,
+            out_specs=(pl.BlockSpec(memory_space=pl.ANY),) * 2,
+            scratch_shapes=[pltpu.VMEM(r.shape, r.dtype) for r in results] + [pltpu.SemaphoreType.DMA((4,))],
+            name="hand_on",
+        )(*results)
 
     row_spec = P(("batch", "rows"), None)
     out_spec = P("batch", None)

time: 121 us -> 120 us (level)
  local copies, waits for them, and re-layouts: 3.93 us -> 0 us
  Pallas kernels: 117 us -> 119 us
    unnamed x2 -> x0, local copies, waits for them, and re-layouts: 3.93 us -> none
    pallas_call x0 -> x1, Pallas kernels: none -> 2.32 us  [group_solve(): pl.pallas_call(hand_on, out_shape=tuple((jax.ShapeDtypeStruct(r.shape, r....]
where the time goes in v6:
time: 120 us; the launch traced here: 119 us
  Pallas kernels  119 us (99%)
    pallas_call x1, Pallas kernels, group_solve(): pl.pallas_call(solve_kernel, out_shape=(jax.ShapeDtypeStruct((512, 128),...  116 us

profile of v6, /device:TPU:1, one launch (start us, length us, event | category | flops | bytes accessed | tf_op | source)
XLA Modules:
  0.0 119.5 jit_solution(17726962157884446226)
XLA Ops:
  0.6 116.3 %solve.1 = (f32[512,128]{1,0:T(8,128)}, f32[512,512]{1,0:T(8,128)}) custom-call(f32[4096,512]{1,0:T(8,128)} %a_hbm.1, f32[4096,128]{1,0:T(8,128)} %b_hbm.1), custom_call_target="tpu_custom_call" | custom-call | tf_op jit(solution)/shard_map/solve/pallas_call | solution.py:368
  117.0 2.3 %hand_on.1 = (f32[512,128]{1,0:T(8,128)}, f32[512,512]{1,0:T(8,128)}) custom-call(f32[512,128]{1,0:T(8,128)} %get-tuple-element.4.x_in, f32[512,512]{1,0:T(8,128)} %get-tuple-element.5.r_in), custom_call_target="tpu_custom_call" | custom-call | tf_op jit(solution)/shard_map/hand_on/pallas_call | solution.py:381

commit v7 on v6

--- a/solution.py
+++ b/solution.py
@@ -137,101 +137,93 @@
     lane = lax.broadcasted_iota(jnp.int32, (8, 128), 1)
     d_row = lax.broadcasted_iota(jnp.int32, (128, 128), 0)
     d_col = lax.broadcasted_iota(jnp.int32, (128, 128), 1)
-    d_mat = jnp.where(d_col >= d_row, d_mat, d_mat.T)
-    rows = [d_mat[8 * i:8 * i + 8, :] for i in range(16)]
-    inv = [jnp.where(lane == sub + 8 * i, 1.0, 0.0).astype(jnp.float32) for i in range(16)]
+    rows = jnp.where(d_col >= d_row, d_mat, d_mat.T).reshape(16, 8, 128)
+    inv = jnp.where(d_col == d_row, 1.0, 0.0).astype(jnp.float32).reshape(16, 8, 128)
+
+    def spread(v, r):
+        return jnp.broadcast_to(v[r:r + 1, :], (8, 128))
     r_out, v_out = [], []
     for k in range(16):
-        cols = {i: [jnp.broadcast_to(rows[i][:, 8 * k + r:8 * k + r + 1], (8, 128)) for r in range(8)] for i in range(k, 16)}
+        n = 15 - k
+        row_k, inv_k = rows[0], inv[0]
+        top = [jnp.broadcast_to(row_k[:, 8 * k + r:8 * k + r + 1], (8, 128)) for r in range(8)]
+        if n:
+            rows, inv = rows[1:], inv[1:]
+            cols = [jnp.broadcast_to(rows[:, :, 8 * k + r:8 * k + r + 1], (n, 8, 128)) for r in range(8)]
         scale = jnp.zeros((8, 128), jnp.float32)
-        top = cols[k]
         for r in range(8):
-            inv_root = lax.rsqrt(jnp.broadcast_to(top[r][r:r + 1, :], (8, 128)))
+            inv_root = lax.rsqrt(spread(top[r], r))
             scale = jnp.where(sub == r, inv_root, scale)
             below = jnp.where(sub > r, top[r] * inv_root, 0.0)
-            row_s = jnp.broadcast_to(rows[k][r:r + 1, :], (8, 128)) * inv_root
-            row_v = jnp.broadcast_to(inv[k][r:r + 1, :], (8, 128)) * inv_root
-            coef = [jnp.broadcast_to(top[c][r:r + 1, :], (8, 128)) * inv_root for c in range(r + 1, 8)]
+            row_s = spread(row_k, r) * inv_root
+            row_v = spread(inv_k, r) * inv_root
+            coef = [spread(top[c], r) * inv_root for c in range(r + 1, 8)]
             for c in range(r + 1, 8):
                 top[c] = top[c] - below * coef[c - r - 1]
-            rows[k] = rows[k] - below * row_s
-            inv[k] = inv[k] - below * row_v
-            for i in range(k + 1, 16):
-                mult = cols[i][r] * inv_root
+            row_k = row_k - below * row_s
+            inv_k = inv_k - below * row_v
+            if n:
+                mult = cols[r] * inv_root
                 for c in range(r + 1, 8):
-                    cols[i][c] = cols[i][c] - mult * coef[c - r - 1]
-                rows[i] = rows[i] - mult * row_s
-                inv[i] = inv[i] - mult * row_v
-        r_out.append(jnp.where(lane >= sub + 8 * k, rows[k] * scale, 0.0))
-        v_out.append(inv[k] * scale)
+                    cols[c] = cols[c] - mult * coef[c - r - 1]
+                rows = rows - mult * row_s
+                inv = inv - mult * row_v
+        r_out.append(jnp.where(lane >= sub + 8 * k, row_k * scale, 0.0))
+        v_out.append(inv_k * scale)
     return r_out, v_out
 
 
-def factor(pieces, r_mat, x_out, s_mat, v_mat):
-    width = s_mat.shape[1]
+def factor(pieces, r_mat, x_out, s_mat, v_mat, beside, hooks):
     p_lo, p_mid, p_hi = pieces
-    s_mat[256:, 256:] = jnp.zeros((256, width - 256), jnp.float32)
-    p_lo.finish()
-    for t, (j, i) in enumerate(LOLO):
-        block(s_mat, j, i)[...] = piece_block(p_lo.o, t)
-    if width > 512:
-        for t in range(2):
-            block(s_mat, t, 4)[...] = piece_block(p_lo.o, 3 + t).T
-
-    @pl.loop(0, 4)
-    def _(j):
-        top = pl.multiple_of(j * 128, 128)
-
-        @pl.when(j == 2)
-        def _():
-            p_hi.finish()
-            for t, (jj, ii) in enumerate(HIHI):
-                block(s_mat, jj, ii)[...] += piece_block(p_hi.o, t)
-            if width > 512:
-                for t in range(2):
-                    block(s_mat, 2 + t, 4)[...] += piece_block(p_hi.o, 3 + t).T
-        r_blk, v_blk = factor_block(s_mat[pl.ds(top, 128), pl.ds(top, 128)])
-        for i in range(16):
-            r_mat[pl.ds(top + 8 * i, 8), pl.ds(top, 128)] = r_blk[i]
-            v_mat[pl.ds(top + 8 * i, 8), :] = v_blk[i]
-
-        @pl.when(j == 0)
-        def _():
-            p_mid.spread()
-            p_hi.gather()
-            p_mid.finish()
-            for t, (jj, ii) in enumerate(LOHI):
-                block(s_mat, jj, ii)[...] = piece_block(p_mid.o, t)
-
-        @pl.when(j == 1)
-        def _():
-            p_hi.spread()
-        for jj in range(4):
-            lo, hi = 128 * jj, 128 * jj + 128
-            if hi < width:
-                @pl.when(j == jj)
-                def _():
-                    row = mm(v_mat[lo:hi, :], s_mat[lo:hi, hi:])
-                    r_mat[lo:hi, hi:] = row
-                    if hi < 512:
-                        s_mat[hi:, hi:] = s_mat[hi:, hi:] - mm_t(row[:, :512 - hi], row)
     for jj in range(1, 4):
         r_mat[128 * jj:128 * jj + 128, :128 * jj] = jnp.zeros((128, 128 * jj), jnp.float32)
+    x_out[256:, :256] = jnp.zeros((256, 256), jnp.float32)
+    p_lo.finish()
+    for t, ij in enumerate(LOLO):
+        block(s_mat, *ij)[...] = piece_block(p_lo.o, t)
+
     for p in range(2):
         lo, mid, hi = 256 * p, 256 * p + 128, 256 * p + 256
+        if p == 1:
+            for t, ij in enumerate(LOHI):
+                block(s_mat, *ij)[...] = piece_block(p_mid.o, t)
+            right = mm_t(x_out[:256, :256], s_mat[:256, 256:])
+            r_mat[:256, 256:] = right
+            s_mat[256:, 256:] = mm_t(right, right)
+            p_hi.finish()
+            for t, ij in enumerate(HIHI):
+                block(s_mat, *ij)[...] = piece_block(p_hi.o, t) - block(s_mat, *ij)[...]
+
+        @pl.loop(0, 2)
+        def _(j):
+            top = pl.multiple_of(lo + j * 128, 128)
+            r_blk, v_blk = factor_block(s_mat[pl.ds(top, 128), pl.ds(top, 128)])
+            if p == 1:
+                beside(j)
+            for i in range(16):
+                r_mat[pl.ds(top + 8 * i, 8), pl.ds(top, 128)] = r_blk[i]
+                v_mat[pl.ds(top + 8 * i, 8), :] = v_blk[i]
+            for jj in range(2):
+                if (p, jj) in hooks:
+                    pl.when(j == jj)(hooks[p, jj])
+
+            @pl.when(j == 0)
+            def _():
+                row = mm(v_mat[lo:mid, :], s_mat[lo:mid, mid:hi])
+                r_mat[lo:mid, mid:hi] = row
+                s_mat[mid:hi, mid:hi] = s_mat[mid:hi, mid:hi] - mm_t(row, row)
         x_lo, x_hi = v_mat[lo:mid, :].T, v_mat[mid:hi, :].T
         x_out[lo:mid, lo:mid] = x_lo
         x_out[mid:hi, mid:hi] = x_hi
         x_out[mid:hi, lo:mid] = jnp.zeros((128, 128), jnp.float32)
         x_out[lo:mid, mid:hi] = -mm(x_lo, mm(r_mat[lo:mid, mid:hi], x_hi))
-    x_out[256:, :256] = jnp.zeros((256, 256), jnp.float32)
-    x_out[:256, 256:] = -mm(mm(x_out[:256, :256], r_mat[:256, 256:512]), x_out[256:, 256:])
+    x_out[:256, 256:] = -mm(mm(x_out[:256, :256], r_mat[:256, 256:]), x_out[256:, 256:])
 
 
 def solve_kernel(a_hbm, b_hbm, sol, r_fac, a_buf, q_lo, b_buf, acc, proj, *refs):
-    piece_refs, (s_one, v_one, r_one, x_one, s_two, v_two, r_two, x_two, load_sem) = refs[:42], refs[42:]
+    piece_refs, (s_one, v_one, r_one, x_one, s_two, v_two, r_two, x_two, load_sem) = refs[:49], refs[49:]
     one = [Piece(piece_refs[7 * p:7 * p + 7], off) for p, off in enumerate((0, 24, 56))]
-    two = [Piece(piece_refs[7 * p:7 * p + 7], off) for p, off in zip((3, 4, 5), (0, 40, 72))]
+    two = [Piece(piece_refs[7 * p:7 * p + 7], off) for p, off in zip((3, 4, 5, 6), (0, 24, 56, 16))]
     rows = a_hbm.shape[0]
     steps = rows // TILE
 
@@ -250,11 +242,11 @@
     acc[...] = jnp.zeros_like(acc)
     proj[...] = jnp.zeros_like(proj)
 
-    @pl.loop(0, rows // WIDE)
-    def _(i):
-        for part in range(WIDE // LOAD):
-            load_a(i * (WIDE // LOAD) + part).wait()
-        a_lo = a_buf[tile(i, WIDE), :256]
+    @pl.loop(0, steps)
+    def _(i):
+        for part in range(TILE // LOAD):
+            load_a(i * (TILE // LOAD) + part).wait()
+        a_lo = a_buf[tile(i), :256]
         acc[:256, :256] += mm_t(a_lo, a_lo)
     pack(one[0].x, [block(acc, *ij) for ij in LOLO])
     pl.semaphore_wait(barrier, CHIPS)
@@ -281,24 +273,31 @@
             one[1].scatter()
     pack(one[2].x, [block(acc, *ij) for ij in HIHI])
     one[2].start()
-    one[0].spread()
     one[2].scatter()
     one[1].gather()
-    factor(one, r_one, x_one, s_one, v_one)
+    one[0].spread()
+
+    def q_left(j):
+        q_lo[tile(j, WIDE), :] = mm(a_buf[tile(j, WIDE), :256], x_one[:256, :256])
+
+    def arrive(p_mid, p_hi):
+        p_hi.gather()
+        p_mid.spread()
+
+    def arrived(p_mid, p_hi):
+        p_mid.finish()
+        p_hi.spread()
+    factor(one, r_one, x_one, s_one, v_one, q_left,
+           {(0, 0): lambda: arrive(one[1], one[2]), (0, 1): lambda: arrived(one[1], one[2])})
 
     acc[...] = jnp.zeros_like(acc)
     load_b.wait()
 
     @pl.loop(0, rows // WIDE)
     def _(i):
-        q_lo[tile(i, WIDE), :] = mm(a_buf[tile(i, WIDE), :256], x_one[:256, :256])
-
-    @pl.loop(0, rows // WIDE)
-    def _(i):
         q_blk = q_lo[tile(i, WIDE), :]
         acc[:256, :256] += mm_t(q_blk, q_blk)
-        proj[:, :256] += mm_t(b_buf[tile(i, WIDE), :], q_blk)
-    pack(two[0].x, [block(acc, *ij) for ij in LOLO] + [block(proj, 0, i) for i in range(2)])
+    pack(two[0].x, [block(acc, *ij) for ij in LOLO])
     two[0].start()
 
     @pl.loop(0, steps)
@@ -323,26 +322,45 @@
     def _(i):
         q_hi = a_buf[tile(i), 256:]
         acc[256:, 256:] += mm_t(q_hi, q_hi)
-        proj[:, 256:] += mm_t(b_buf[tile(i), :], q_hi)
 
         @pl.when(i == 0)
         def _():
             two[1].scatter()
-
-        @pl.when(i == 2)
-        def _():
+    pack(two[2].x, [block(acc, *ij) for ij in HIHI])
+    two[2].start()
+
+    @pl.loop(0, steps)
+    def _(i):
+        b_blk = b_buf[tile(i), :]
+        proj[:, :256] += mm_t(b_blk, q_lo[tile(i), :])
+        proj[:, 256:] += mm_t(b_blk, a_buf[tile(i), 256:])
+
+        @pl.when(i == 1)
+        def _():
+            two[2].scatter()
             two[0].spread()
-    pack(two[2].x, [block(acc, *ij) for ij in HIHI] + [block(proj, 0, i) for i in range(2, 4)])
-    two[2].start()
+    pack(two[3].x, [block(proj, 0, i) for i in range(4)])
+    two[3].start()
     two[1].gather()
-    two[2].scatter()
-    factor(two, r_two, x_two, s_two, v_two)
-
-    sol[...] = mm(x_one[...], mm(x_two[...], r_two[:, 512:]))
-    r_fac[:256, :256] = mm(r_two[:256, :256], r_one[:256, :256])
-    r_fac[:256, 256:] = mm(r_two[:256, :512], r_one[:, 256:])
-    r_fac[256:, 256:] = mm(r_two[256:, 256:512], r_one[256:, 256:])
+
+    def rows_of_r(j):
+        at = pl.ds(pl.multiple_of(j * 128, 128), 128)
+        r_fac[at, :] = mm(r_two[at, :], r_one[...])
+
+    def arrive_two():
+        arrive(two[1], two[2])
+        two[3].scatter()
+
+    def arrived_two():
+        arrived(two[1], two[2])
+        two[3].gather()
+    factor(two[:3], r_two, x_two, s_two, v_two, rows_of_r, {(0, 0): arrive_two, (0, 1): arrived_two, (1, 0): two[3].spread})
     r_fac[256:, :256] = jnp.zeros((256, 256), jnp.float32)
+    r_fac[256:, 256:] = mm(r_two[256:, 256:], r_one[256:, 256:])
+    two[3].finish()
+    for t in range(4):
+        proj[:, t * 128:t * 128 + 128] = piece_block(two[3].o, t)
+    sol[...] = mm(x_one[...], mm(x_two[...], mm(proj[...], x_two[...]).T))
 
 
 def hand_on(x_in, r_in, x_out, r_out, x_buf, r_buf, sems):
@@ -371,9 +389,9 @@
             in_specs=[pl.BlockSpec(memory_space=pl.ANY)] * 2,
             out_specs=(pl.BlockSpec(memory_space=pltpu.VMEM),) * 2,
             scratch_shapes=[buf(rows, 512), buf(rows, 256), buf(rows), buf(512, 512), buf(128, 512),
-                            *piece(384), *piece(512), *piece(384), *piece(640), *piece(512), *piece(640),
+                            *piece(384), *piece(512), *piece(384), *piece(384), *piece(512), *piece(384), *piece(512),
                             buf(512, 512), buf(512), buf(512, 512), buf(512, 512),
-                            buf(512, 640), buf(512), buf(512, 640), buf(512, 512),
+                            buf(512, 512), buf(512), buf(512, 512), buf(512, 512),
                             pltpu.SemaphoreType.DMA((rows // LOAD + 1,))],
             compiler_params=pltpu.CompilerParams(collective_id=0, has_side_effects=True, vmem_limit_bytes=GIVE),
             name="solve",

time: 120 us -> 114 us (0.950)
  Pallas kernels: 119 us -> 112 us
    pallas_call x1, Pallas kernels: 116 us -> 110 us  [group_solve(): pl.pallas_call(solve_kernel, out_shape=(jax.ShapeDtypeStruct((512, 128),...]
where the time goes in v7:
time: 114 us; the launch traced here: 113 us
  Pallas kernels  112 us (98%)
    pallas_call x1, Pallas kernels, group_solve(): pl.pallas_call(solve_kernel, out_shape=(jax.ShapeDtypeStruct((512, 128),...  110 us
    pallas_call x1, Pallas kernels, group_solve(): pl.pallas_call(hand_on, out_shape=tuple((jax.ShapeDtypeStruct(r.shape, r....  2.32 us

profile of v7, /device:TPU:1, one launch (start us, length us, event | category | flops | bytes accessed | tf_op | source)
XLA Modules:
  0.0 112.7 jit_solution(14098911571566267714)
XLA Ops:
  0.6 109.5 %solve.1 = (f32[512,128]{1,0:T(8,128)}, f32[512,512]{1,0:T(8,128)}) custom-call(f32[4096,512]{1,0:T(8,128)} %a_hbm.1, f32[4096,128]{1,0:T(8,128)} %b_hbm.1), custom_call_target="tpu_custom_call" | custom-call | tf_op jit(solution)/shard_map/solve/pallas_call | solution.py:386
  110.1 2.3 %hand_on.1 = (f32[512,128]{1,0:T(8,128)}, f32[512,512]{1,0:T(8,128)}) custom-call(f32[512,128]{1,0:T(8,128)} %get-tuple-element.4.x_in, f32[512,512]{1,0:T(8,128)} %get-tuple-element.5.r_in), custom_call_target="tpu_custom_call" | custom-call | tf_op jit(solution)/shard_map/hand_on/pallas_call | solution.py:399

commit v8 on v7

--- a/solution.py
+++ b/solution.py
@@ -200,6 +200,7 @@
             r_blk, v_blk = factor_block(s_mat[pl.ds(top, 128), pl.ds(top, 128)])
             if p == 1:
                 beside(j)
+                s_mat[:256, :256] = mm(x_out[:256, :256], r_mat[:256, 256:])
             for i in range(16):
                 r_mat[pl.ds(top + 8 * i, 8), pl.ds(top, 128)] = r_blk[i]
                 v_mat[pl.ds(top + 8 * i, 8), :] = v_blk[i]
@@ -217,7 +218,7 @@
         x_out[mid:hi, mid:hi] = x_hi
         x_out[mid:hi, lo:mid] = jnp.zeros((128, 128), jnp.float32)
         x_out[lo:mid, mid:hi] = -mm(x_lo, mm(r_mat[lo:mid, mid:hi], x_hi))
-    x_out[:256, 256:] = -mm(mm(x_out[:256, :256], r_mat[:256, 256:]), x_out[256:, 256:])
+    x_out[:256, 256:] = -mm(s_mat[:256, :256], x_out[256:, 256:])
 
 
 def solve_kernel(a_hbm, b_hbm, sol, r_fac, a_buf, q_lo, b_buf, acc, proj, *refs):
@@ -274,8 +275,8 @@
     pack(one[2].x, [block(acc, *ij) for ij in HIHI])
     one[2].start()
     one[2].scatter()
+    one[0].spread()
     one[1].gather()
-    one[0].spread()
 
     def q_left(j):
         q_lo[tile(j, WIDE), :] = mm(a_buf[tile(j, WIDE), :256], x_one[:256, :256])

time: 114 us -> 114 us (level)
  no operation moved by 1% of the time
where the time goes in v8:
time: 114 us; the launch traced here: 113 us
  Pallas kernels  112 us (98%)
    pallas_call x1, Pallas kernels, group_solve(): pl.pallas_call(solve_kernel, out_shape=(jax.ShapeDtypeStruct((512, 128),...  109 us
    pallas_call x1, Pallas kernels, group_solve(): pl.pallas_call(hand_on, out_shape=tuple((jax.ShapeDtypeStruct(r.shape, r....  2.32 us

profile of v8, /device:TPU:1, one launch (start us, length us, event | category | flops | bytes accessed | tf_op | source)
XLA Modules:
  0.0 112.5 jit_solution(14727058783105750583)
XLA Ops:
  0.6 109.3 %solve.1 = (f32[512,128]{1,0:T(8,128)}, f32[512,512]{1,0:T(8,128)}) custom-call(f32[4096,512]{1,0:T(8,128)} %a_hbm.1, f32[4096,128]{1,0:T(8,128)} %b_hbm.1), custom_call_target="tpu_custom_call" | custom-call | tf_op jit(solution)/shard_map/solve/pallas_call | solution.py:387
  110.0 2.3 %hand_on.1 = (f32[512,128]{1,0:T(8,128)}, f32[512,512]{1,0:T(8,128)}) custom-call(f32[512,128]{1,0:T(8,128)} %get-tuple-element.4.x_in, f32[512,512]{1,0:T(8,128)} %get-tuple-element.5.r_in), custom_call_target="tpu_custom_call" | custom-call | tf_op jit(solution)/shard_map/hand_on/pallas_call | solution.py:400
